TPU v7x, 8 devices: a whole 2x2x1 slice. The times are simulated.
8 devices in a mesh: dp: 1 (over z), cp: 8 (over y, x, core).
Axes of the slice: x: 2, y: 2, z: 1, core: 2. Of those that a mesh axis runs over, the one named last changes fastest.
Arguments:
- hidden: bfloat16 [3, 1024, 2560], P('dp', 'cp')
- positions: int32 [3, 1024], P('dp', 'cp')
- wq_local: bfloat16 [2560, 2048], replicated
- wk_local: bfloat16 [2560, 1024], replicated
- wv_local: bfloat16 [2560, 1024], replicated
- wo_local: bfloat16 [2048, 2560], replicated
- wgate_local: bfloat16 [2560, 10240], replicated
- wup_local: bfloat16 [2560, 10240], replicated
- wdown_local: bfloat16 [10240, 2560], replicated
- preatt_local: float32 [2560], replicated
- postatt_local: float32 [2560], replicated
- preffw_local: float32 [2560], replicated
- postffw_local: float32 [2560], replicated
- wq_global: bfloat16 [2560, 2048], replicated
- wk_global: bfloat16 [2560, 1024], replicated
- wv_global: bfloat16 [2560, 1024], replicated
- wo_global: bfloat16 [2048, 2560], replicated
- wgate_global: bfloat16 [2560, 10240], replicated
- wup_global: bfloat16 [2560, 10240], replicated
- wdown_global: bfloat16 [10240, 2560], replicated
- preatt_global: float32 [2560], replicated
- postatt_global: float32 [2560], replicated
- preffw_global: float32 [2560], replicated
- postffw_global: float32 [2560], replicated
Outputs:
- output: bfloat16 [3, 1024, 2560], P('dp', 'cp')
All inputs are finite; a program needn't handle non-finite values.
Results may differ from a plain program's by a relative error of at most 0.02.
Values are sent between devices in bfloat16 or wider.
A program may use at most 1.5 GiB of HBM per device.

v0:
```python
import jax
import jax.numpy as jnp
from jax import lax
from jax.sharding import PartitionSpec as P

HEAD_DIM = 256
WINDOW = 512
EPSILON = 1e-6
THETA = 10000.0
SOFT_CAP = 50.0


def rms_norm(inputs, norm_scale):
    widened = inputs.astype(jnp.float32)
    mean_sq = jnp.mean(widened * widened, axis=-1, keepdims=True)
    return (widened * lax.rsqrt(mean_sq + EPSILON) * (1.0 + norm_scale)).astype(jnp.bfloat16)


def rope_tables(tok_pos):
    half_dim = HEAD_DIM // 2
    inv_freq = THETA ** (-(jnp.arange(half_dim, dtype=jnp.float32) * 2.0 / HEAD_DIM))
    angles = tok_pos.astype(jnp.float32)[:, :, None, None] * inv_freq
    return jnp.cos(angles), jnp.sin(angles)


def apply_rope(heads_in, cos_t, sin_t):
    half_dim = HEAD_DIM // 2
    widened = heads_in.astype(jnp.float32)
    first_half = widened[..., :half_dim]
    second_half = widened[..., half_dim:]
    return jnp.concatenate([first_half * cos_t - second_half * sin_t, second_half * cos_t + first_half * sin_t], axis=-1)


def project_qkv(hidden, cos_t, sin_t, weights):
    w_q, w_k, w_v, pre_att = weights[0], weights[1], weights[2], weights[7]
    batch_rows, tok_len = hidden.shape[0], hidden.shape[1]
    kv_heads = w_k.shape[1] // HEAD_DIM
    group_size = w_q.shape[1] // w_k.shape[1]
    normed = rms_norm(hidden, pre_att)
    q_raw = jnp.einsum("btd,dn->btn", normed, w_q, preferred_element_type=jnp.float32).astype(jnp.bfloat16)
    k_raw = jnp.einsum("btd,dn->btn", normed, w_k, preferred_element_type=jnp.float32).astype(jnp.bfloat16)
    v_raw = jnp.einsum("btd,dn->btn", normed, w_v, preferred_element_type=jnp.float32).astype(jnp.bfloat16)
    query_rot = apply_rope(q_raw.reshape(batch_rows, tok_len, kv_heads * group_size, HEAD_DIM), cos_t, sin_t)
    query_rot = (query_rot * HEAD_DIM ** -0.5).astype(jnp.bfloat16).reshape(batch_rows, tok_len, kv_heads, group_size, HEAD_DIM)
    key_rot = apply_rope(k_raw.reshape(batch_rows, tok_len, kv_heads, HEAD_DIM), cos_t, sin_t).astype(jnp.bfloat16)
    value_t = v_raw.reshape(batch_rows, tok_len, kv_heads, HEAD_DIM)
    return query_rot, key_rot, value_t


def attend(query_rot, key_all, value_all, q_pos, k_pos, window_len):
    scores = jnp.einsum("btkgd,bskd->bkgts", query_rot, key_all, preferred_element_type=jnp.float32)
    capped = SOFT_CAP * jnp.tanh(scores / SOFT_CAP)
    offset = q_pos[:, None, None, :, None] - k_pos[:, None, None, None, :]
    visible = (offset >= 0) & (offset < window_len)
    prob_bf = jax.nn.softmax(jnp.where(visible, capped, -1e30), axis=-1).astype(jnp.bfloat16)
    mixed_heads = jnp.einsum("bkgts,bskd->btkgd", prob_bf, value_all, preferred_element_type=jnp.float32).astype(jnp.bfloat16)
    return mixed_heads.reshape(query_rot.shape[0], query_rot.shape[1], -1)


def finish_layer(hidden, mixed_heads, weights):
    w_o, w_gate, w_up, w_down = weights[3], weights[4], weights[5], weights[6]
    post_att, pre_ffw, post_ffw = weights[8], weights[9], weights[10]
    attn_out = jnp.einsum("btn,nd->btd", mixed_heads, w_o, preferred_element_type=jnp.float32).astype(jnp.bfloat16)
    mid_state = (hidden.astype(jnp.float32) + rms_norm(attn_out, post_att).astype(jnp.float32)).astype(jnp.bfloat16)
    normed_mid = rms_norm(mid_state, pre_ffw)
    gate_val = jnp.einsum("btd,df->btf", normed_mid, w_gate, preferred_element_type=jnp.float32).astype(jnp.bfloat16)
    up_val = jnp.einsum("btd,df->btf", normed_mid, w_up, preferred_element_type=jnp.float32).astype(jnp.bfloat16)
    act_val = (jax.nn.gelu(gate_val.astype(jnp.float32), approximate=True) * up_val.astype(jnp.float32)).astype(jnp.bfloat16)
    down_val = jnp.einsum("btf,fd->btd", act_val, w_down, preferred_element_type=jnp.float32).astype(jnp.bfloat16)
    return (mid_state.astype(jnp.float32) + rms_norm(down_val, post_ffw).astype(jnp.float32)).astype(jnp.bfloat16)


def solution(mesh):
    cp_size = mesh.shape["cp"]

    def device_step(hidden, positions, *weights):
        local_w = weights[:11]
        global_w = weights[11:]
        chunk_len = hidden.shape[1]
        my_index = lax.axis_index("cp")
        all_pos = lax.all_gather(positions, "cp", axis=1, tiled=True)
        cos_t, sin_t = rope_tables(positions)
        n_prev = (WINDOW + chunk_len - 2) // chunk_len
        query_rot, key_rot, value_t = project_qkv(hidden, cos_t, sin_t, local_w)
        key_parts = [key_rot]
        value_parts = [value_t]
        pos_parts = [positions]
        for shift_by in range(1, n_prev + 1):
            perm_pairs = [(source_idx, source_idx + shift_by) for source_idx in range(cp_size - shift_by)]
            key_parts.append(lax.ppermute(key_rot, "cp", perm_pairs))
            value_parts.append(lax.ppermute(value_t, "cp", perm_pairs))
            start_at = ((my_index - shift_by) % cp_size) * chunk_len
            pos_parts.append(lax.dynamic_slice_in_dim(all_pos, start_at, chunk_len, axis=1))
        mixed_heads = attend(query_rot, jnp.concatenate(key_parts, axis=1), jnp.concatenate(value_parts, axis=1), positions, jnp.concatenate(pos_parts, axis=1), WINDOW)
        mid_hidden = finish_layer(hidden, mixed_heads, local_w)
        query_rot, key_rot, value_t = project_qkv(mid_hidden, cos_t, sin_t, global_w)
        key_all = lax.all_gather(key_rot, "cp", axis=1, tiled=True)
        value_all = lax.all_gather(value_t, "cp", axis=1, tiled=True)
        mixed_heads = attend(query_rot, key_all, value_all, positions, all_pos, 2 * chunk_len * cp_size)
        return finish_layer(mid_hidden, mixed_heads, global_w)

    specs_in = tuple([P("dp", "cp"), P("dp", "cp")] + [P()] * 22)
    return jax.shard_map(device_step, mesh=mesh, in_specs=specs_in, out_specs=P("dp", "cp"), check_vma=False)
```

profile of v0, /device:TPU:0, one launch (start us, length us, event | category | flops | bytes accessed | tf_op | source)
XLA Modules:
  0.0 519.3 jit_solution(253096063371907129)
XLA Ops:
  7.8 2.0 fusion.110
  9.8 5.3 %fusion.171 = f32[3,128,1024]{2,1,0:T(8,128)S(1)} fusion(bf16[2560,1024]{1,0:T(8,128)(2,1)} %param.27, bf16[3,128,2560]{2,1,0:T(8,128)(2,1)} %param.24, f32[2560]{0:T(1024)S(1)} %broadcast_add_fusion.7, f32[3,128]{1,0:T(4,128)S(1)} %add_rsqrt_fusion.7), kind=kOutput, calls=%fused_computation.163 | convolution fusion | flops 2017984512 | bytes 8793600 | tf_op jit(solution)/shard_map/btd,dn->btn/dot_general | solution.py:41
  16.8 1.4 multiply_cosine_fusion
  20.5 3.8 collective-permute-start.4
  24.3 4.4 collective-permute-start.5
  28.7 4.3 collective-permute-start.6
  33.0 2.2 collective-permute-start.7
  35.2 4.7 fusion.165
  41.1 2.2 collective-permute-start
  43.4 56.1 %all_gather.9 = s32[3,1024]{1,0:T(4,128)S(1)} all-gather(s32[3,128]{1,0:T(4,128)S(1)} %copy-done.17), channel_id=1, replica_groups=mesh['dp'=1,'cp'=8] {'cp'}, dimensions={1}, use_global_device_ids=true | all-gather | bytes 13824 | tf_op jit(solution)/shard_map/all_gather | solution.py:81
  99.6 7.0 %fusion.139 = f32[3,128,2048]{2,1,0:T(8,128)S(1)} fusion(bf16[2560,2048]{1,0:T(8,128)(2,1)} %param.26, bf16[3,128,2560]{2,1,0:T(8,128)(2,1)S(1)} %copy-done.1, f32[2560]{0:T(1024)} %copy-done.23, f32[3,128]{1,0:T(4,128)S(1)} %copy-done.29), kind=kOutput, calls=%fused_computation.145 | convolution fusion | flops 4032036864 | bytes 15609344 | tf_op jit(solution)/shard_map/btd,dn->btn/dot_general | solution.py:40
  106.6 1.4 copy.74
  108.1 1.5 multiply_subtract_fusion.1
  115.6 1.8 copy.49
  122.2 4.5 collective-permute-start.2
  127.9 2.1 collective-permute-start.3
  133.8 2.9 collective-permute-done.1
  138.1 7.8 %collective-permute-done.2 = bf16[3,128,4,256]{1,3,2,0:T(8,128)(2,1)S(1)} collective-permute-done((bf16[3,128,4,256]{1,3,2,0:T(8,128)(2,1)}, bf16[3,128,4,256]{1,3,2,0:T(8,128)(2,1)S(1)}, u32[]{:S(2)}, u32[]{:S(2)}) %collective-permute-start.2) | collective-permute-done | bytes 786464 | tf_op jit(solution)/shard_map/ppermute | solution.py:91
  146.2 6.4 %fusion.220 = (f32[3,4,2,128]{3,2,1,0:T(2,128)S(1)}, f32[3,4,2,128,640]{3,4,2,1,0:T(8,128)}) fusion(f32[3,4,640,128,2]{3,2,4,1,0:T(8,128)S(1)} %fusion.126, pred[3,128,640]{1,2,0:T(8,128)(4,1)S(1)} %fusion.189), kind=kOutput, calls=%fused_computation.232 | output fusion | flops 15729279 | bytes 15986688 | tf_op jit(solution)/shard_map/sub | solution.py:55
  152.5 11.6 %collective-permute-done.3 = bf16[3,128,4,256]{1,3,2,0:T(8,128)(2,1)S(1)} collective-permute-done((bf16[3,128,4,256]{1,3,2,0:T(8,128)(2,1)}, bf16[3,128,4,256]{1,3,2,0:T(8,128)(2,1)S(1)}, u32[]{:S(2)}, u32[]{:S(2)}) %collective-permute-start.3) | collective-permute-done | bytes 786464 | tf_op jit(solution)/shard_map/ppermute | solution.py:91
  164.4 4.7 fusion.148
  169.1 8.4 %fusion.98 = (f32[3,128]{1,0:T(4,128)S(1)}, bf16[3,128,2560]{2,1,0:T(8,128)(2,1)S(1)}) fusion(bf16[3,128,2048]{1,2,0:T(8,128)(2,1)S(1)} %bitcast.197, bf16[2048,2560]{1,0:T(8,128)(2,1)} %param.29), kind=kOutput, calls=%fused_computation.104 | convolution fusion | flops 4030463488 | bytes 14026240 | tf_op jit(solution)/shard_map/btn,nd->btd/dot_general | solution.py:63
  177.5 2.3 fusion.114
  179.8 35.1 %fusion.28 = bf16[3,128,10240]{2,1,0:T(8,128)(2,1)} fusion(bf16[2560,10240]{1,0:T(8,128)(2,1)} %param.30, bf16[3,128,2560]{2,1,0:T(8,128)(2,1)} %get-tuple-element.10, f32[2560]{0:T(1024)S(1)} %broadcast_add_fusion.5, f32[3,128]{1,0:T(4,128)S(1)} %add_rsqrt_fusion.5), kind=kOutput, calls=%fused_computation.36 | convolution fusion | flops 20140523520 | bytes 62270976 | tf_op jit(solution)/shard_map/btd,df->btf/dot_general | solution.py:66
  215.0 31.8 %fusion.20.clone.3.clone.4 = bf16[3,128,10240]{2,1,0:T(8,128)(2,1)} fusion(bf16[3,128,10240]{2,1,0:T(8,128)(2,1)} %fusion.28, bf16[2560,10240]{1,0:T(8,128)(2,1)} %param.31, bf16[3,128,2560]{2,1,0:T(8,128)(2,1)S(1)} %copy-done.2, f32[2560]{0:T(1024)S(1)} %broadcast_add_fusion.5, f32[3,128]{1,0:T(4,128)S(1)} %add_rsqrt_fusion.5), kind=kOutput, calls=%fused_computation.28.clone.clone.clone.clone.clone.clone.clone.1 | convolution fusion | flops 20187709440 | bytes 70135296 | tf_op jit(solution)/shard_map/btd,df->btf/dot_general | solution.py:67
  246.8 30.8 %fusion.101 = (f32[3,128]{1,0:T(4,128)S(1)}, bf16[3,128,2560]{2,1,0:T(8,128)(2,1)}) fusion(bf16[10240,2560]{1,0:T(8,128)(2,1)} %param.32, bf16[3,128,10240]{2,1,0:T(8,128)(2,1)} %fusion.20.clone.3.clone.4), kind=kOutput, calls=%fused_computation.107 | convolution fusion | flops 20136591360 | bytes 62260736 | tf_op jit(solution)/shard_map/btf,fd->btd/dot_general | solution.py:69
  277.6 3.2 fusion.118
  280.9 5.9 %fusion.180 = f32[3,128,1024]{2,1,0:T(8,128)} fusion(bf16[2560,1024]{1,0:T(8,128)(2,1)} %param.38, bf16[3,128,2560]{2,1,0:T(8,128)(2,1)S(1)} %get-tuple-element.8, f32[2560]{0:T(1024)S(1)} %copy-done.24, f32[3,128]{1,0:T(4,128)S(1)} %add_rsqrt_fusion.3), kind=kOutput, calls=%fused_computation.166 | convolution fusion | flops 2017984512 | bytes 8793600 | tf_op jit(solution)/shard_map/btd,dn->btn/dot_general | solution.py:41
  286.8 1.9 copy.53
  289.9 1.4 copy.73
  291.3 1.4 copy.72
  295.1 4.7 fusion.174
  302.3 1.4 fusion.158
  303.7 7.1 %fusion.145 = f32[3,128,2048]{2,1,0:T(8,128)S(1)} fusion(bf16[2560,2048]{1,0:T(8,128)(2,1)} %param.37, bf16[3,128,2560]{2,1,0:T(8,128)(2,1)S(1)} %get-tuple-element.8, f32[2560]{0:T(1024)S(1)} %copy-done.25, f32[3,128]{1,0:T(4,128)S(1)} %add_rsqrt_fusion.3), kind=kOutput, calls=%fused_computation.147 | convolution fusion | flops 4032036864 | bytes 15609344 | tf_op jit(solution)/shard_map/btd,dn->btn/dot_general | solution.py:40
  310.8 1.4 copy.75
  312.9 1.4 copy.56
  314.3 29.3 %all-gather.5.cloned.1.call-done = bf16[3,1024,4,256]{3,1,2,0:T(8,128)(2,1)} async-done(((bf16[3,128,4,256]{3,1,2,0:T(8,128)(2,1)}), bf16[3,1024,4,256]{3,1,2,0:T(8,128)(2,1)}) %all-gather.5.cloned.1.call-update) | async-done | bytes 6291472 | tf_op jit(solution)/shard_map/all_gather | solution.py:97
  343.6 4.5 fusion.65
  348.1 4.5 copy-done
  352.6 6.8 %fusion.225 = f32[3,4,2,128]{3,2,1,0:T(2,128)S(1)} fusion(f32[3,4,1024,128,2]{3,2,4,1,0:T(8,128)S(1)} %fusion.65, pred[3,128,1024]{1,2,0:T(8,128)(4,1)S(1)} %copy-done.11), kind=kOutput, calls=%fused_computation.233 | output fusion | flops 25166848 | bytes 12988416 | tf_op jit(solution)/shard_map/sub | solution.py:55
  359.4 26.8 %all-gather.3.cloned.1.call-done = bf16[3,1024,4,256]{1,3,2,0:T(8,128)(2,1)} async-done(((bf16[3,128,4,256]{1,3,2,0:T(8,128)(2,1)}), bf16[3,1024,4,256]{1,3,2,0:T(8,128)(2,1)}) %all-gather.3.cloned.1.call-update) | async-done | bytes 6291472 | tf_op jit(solution)/shard_map/all_gather | solution.py:98
  386.2 18.5 %fusion.151 = bf16[3,4,256,2,128]{4,2,3,1,0:T(8,128)(2,1)} fusion(f32[3,4,2,128]{3,2,1,0:T(2,128)S(1)} %fusion.225, bf16[3,1024,4,256]{1,3,2,0:T(8,128)(2,1)} %all-gather.3.cloned.1.call-done, f32[3,4,1024,128,2]{3,2,4,1,0:T(8,128)} %copy-done, pred[3,128,1024]{1,2,0:T(8,128)(4,1)} %fusion.158), kind=kOutput, calls=%fused_computation.151 | convolution fusion | flops 1639714816 | bytes 20852736 | tf_op jit(solution)/shard_map/bkgts,bskd->btkgd/dot_general | solution.py:56
  404.7 8.8 %fusion.104 = (f32[3,128]{1,0:T(4,128)S(1)}, bf16[3,128,2560]{2,1,0:T(8,128)(2,1)S(1)}) fusion(bf16[3,128,2048]{1,2,0:T(8,128)(2,1)} %bitcast.196, bf16[2048,2560]{1,0:T(8,128)(2,1)} %param.40), kind=kOutput, calls=%fused_computation.110 | convolution fusion | flops 4030463488 | bytes 14026240 | tf_op jit(solution)/shard_map/btn,nd->btd/dot_general | solution.py:63
  413.6 2.3 fusion.122
  415.9 30.2 %fusion.34 = bf16[3,128,10240]{2,1,0:T(8,128)(2,1)} fusion(bf16[2560,10240]{1,0:T(8,128)(2,1)} %param.41, bf16[3,128,2560]{2,1,0:T(8,128)(2,1)} %get-tuple-element.6, f32[2560]{0:T(1024)S(1)} %copy-done.26, f32[3,128]{1,0:T(4,128)S(1)} %add_rsqrt_fusion.1), kind=kOutput, calls=%fused_computation.38 | convolution fusion | flops 20140523520 | bytes 62270976 | tf_op jit(solution)/shard_map/btd,df->btf/dot_general | solution.py:66
  446.1 31.9 %fusion.27.clone.3.clone.2 = bf16[3,128,10240]{2,1,0:T(8,128)(2,1)} fusion(bf16[3,128,10240]{2,1,0:T(8,128)(2,1)} %fusion.34, bf16[2560,10240]{1,0:T(8,128)(2,1)} %param.42, bf16[3,128,2560]{2,1,0:T(8,128)(2,1)S(1)} %copy-done.3, f32[2560]{0:T(1024)S(1)} %copy-done.26, f32[3,128]{1,0:T(4,128)S(1)} %add_rsqrt_fusion.1), kind=kOutput, calls=%fused_computation.35.clone.clone.clone.clone.clone.clone.clone | convolution fusion | flops 20187709440 | bytes 70135296 | tf_op jit(solution)/shard_map/btd,df->btf/dot_general | solution.py:67
  478.0 30.3 %fusion.107 = (f32[3,128]{1,0:T(4,128)S(1)}, bf16[3,128,2560]{2,1,0:T(8,128)(2,1)}) fusion(bf16[10240,2560]{1,0:T(8,128)(2,1)} %param.43, bf16[3,128,10240]{2,1,0:T(8,128)(2,1)} %fusion.27.clone.3.clone.2), kind=kOutput, calls=%fused_computation.113 | convolution fusion | flops 20136591360 | bytes 62260736 | tf_op jit(solution)/shard_map/btf,fd->btd/dot_general | solution.py:69
  508.3 3.7 fusion.125
  (114 shorter events, 30.5 us)
Async XLA Ops:
  6.5 337.1 %all-gather.5.cloned.1.call-start = ((), (), s32[]{:S(2)}) async-start(), calls=%async_computation.1 | async-start | bytes 7077888 | tf_op jit(solution)/shard_map/all_gather | solution.py:97
  7.8 27.4 %copy-start.23 = (f32[2560]{0:T(1024)}, f32[2560]{0:T(1024)S(1)}, u32[]{:S(2)}) copy-start(f32[2560]{0:T(1024)S(1)} %broadcast_add_fusion.7) | copy-start | bytes 30724
  9.8 5.3 %copy-start.27 = (f32[3,128]{1,0:T(4,128)}, f32[3,128]{1,0:T(4,128)S(1)}, u32[]{:S(2)}) copy-start(f32[3,128]{1,0:T(4,128)S(1)} %add_rsqrt_fusion.7) | copy-start | bytes 4612
  15.2 1.1 copy-start.16
  15.9 19.2 %copy-start.1 = (bf16[3,128,2560]{2,1,0:T(8,128)(2,1)S(1)}, bf16[3,128,2560]{2,1,0:T(8,128)(2,1)}, u32[]{:S(2)}) copy-start(bf16[3,128,2560]{2,1,0:T(8,128)(2,1)} %param.24) | copy-start | bytes 5898244
  16.0 19.2 %copy-start.28 = (f32[3,128]{1,0:T(4,128)S(1)}, f32[3,128]{1,0:T(4,128)}, u32[]{:S(2)}) copy-start(f32[3,128]{1,0:T(4,128)} %copy-done.27) | copy-start | bytes 4612
  18.2 0.7 copy-start.5
  18.2 0.9 copy-start.8
  20.5 22.9 %copy-start.17 = (s32[3,128]{1,0:T(4,128)S(1)}, s32[3,128]{1,0:T(4,128)}, u32[]{:S(2)}) copy-start(s32[3,128]{1,0:T(4,128)} %param.25) | copy-start | bytes 4612
  20.5 79.1 %copy-start.29 = (f32[3,128]{1,0:T(4,128)S(1)}, f32[3,128]{1,0:T(4,128)}, u32[]{:S(2)}) copy-start(f32[3,128]{1,0:T(4,128)} %copy-done.27) | copy-start | bytes 4612
  20.5 97.9 %collective-permute-start.4 = (bf16[3,128,4,256]{3,1,2,0:T(8,128)(2,1)}, bf16[3,128,4,256]{3,1,2,0:T(8,128)(2,1)}, u32[]{:S(2)}, u32[]{:S(2)}) collective-permute-start(bf16[3,128,4,256]{3,1,2,0:T(8,128)(2,1)} %get-tuple-element.23), channel_id=1, source_target_pairs={{0,1},{1,2},{2,3},{3,4},{4,5},{5,6},{6,7}} | collective-permute-start | bytes 2359304 | tf_op jit(solution)/shard_map/ppermute | solution.py:90
  24.3 97.9 %collective-permute-start.5 = (bf16[3,128,4,256]{3,1,2,0:T(8,128)(2,1)}, bf16[3,128,4,256]{3,1,2,0:T(8,128)(2,1)}, u32[]{:S(2)}, u32[]{:S(2)}) collective-permute-start(bf16[3,128,4,256]{3,1,2,0:T(8,128)(2,1)} %get-tuple-element.23), channel_id=1, source_target_pairs={{0,2},{1,3},{2,4},{3,5},{4,6},{5,7}} | collective-permute-start | bytes 2359304 | tf_op jit(solution)/shard_map/ppermute | solution.py:90
  28.7 99.2 %collective-permute-start.6 = (bf16[3,128,4,256]{3,1,2,0:T(8,128)(2,1)}, bf16[3,128,4,256]{3,1,2,0:T(8,128)(2,1)}, u32[]{:S(2)}, u32[]{:S(2)}) collective-permute-start(bf16[3,128,4,256]{3,1,2,0:T(8,128)(2,1)} %get-tuple-element.23), channel_id=1, source_target_pairs={{0,3},{1,4},{2,5},{3,6},{4,7}} | collective-permute-start | bytes 2359304 | tf_op jit(solution)/shard_map/ppermute | solution.py:90
  33.0 98.2 %collective-permute-start.7 = (bf16[3,128,4,256]{3,1,2,0:T(8,128)(2,1)}, bf16[3,128,4,256]{3,1,2,0:T(8,128)(2,1)}, u32[]{:S(2)}, u32[]{:S(2)}) collective-permute-start(bf16[3,128,4,256]{3,1,2,0:T(8,128)(2,1)} %get-tuple-element.23), channel_id=1, source_target_pairs={{0,4},{1,5},{2,6},{3,7}} | collective-permute-start | bytes 2359304 | tf_op jit(solution)/shard_map/ppermute | solution.py:90
  41.1 91.3 %collective-permute-start = (bf16[3,128,4,256]{1,3,2,0:T(8,128)(2,1)}, bf16[3,128,4,256]{1,3,2,0:T(8,128)(2,1)}, u32[]{:S(2)}, u32[]{:S(2)}) collective-permute-start(bf16[3,128,4,256]{1,3,2,0:T(8,128)(2,1)} %bitcast.34), channel_id=1, source_target_pairs={{0,1},{1,2},{2,3},{3,4},{4,5},{5,6},{6,7}} | collective-permute-start | bytes 2359304 | tf_op jit(solution)/shard_map/ppermute | solution.py:91
  99.5 11.8 %copy-start.12 = (s32[3,1024]{1,0:T(4,128)}, s32[3,1024]{1,0:T(4,128)S(1)}, u32[]{:S(2)}) copy-start(s32[3,1024]{1,0:T(4,128)S(1)} %all_gather.9) | copy-start | bytes 36868
  106.6 1.4 copy-start.6
  106.6 1.4 copy-start.9
  111.3 6.5 %copy-start.19 = (f32[2560]{0:T(1024)S(1)}, f32[2560]{0:T(1024)}, u32[]{:S(2)}) copy-start(f32[2560]{0:T(1024)} %param.44) | copy-start | bytes 30724
  115.6 5.3 %copy-start.4 = (bf16[3,640,4,256]{3,1,2,0:T(8,128)(2,1)S(1)}, bf16[3,640,4,256]{3,1,2,0:T(8,128)(2,1)}, u32[]{:S(2)}) copy-start(bf16[3,640,4,256]{3,1,2,0:T(8,128)(2,1)} %get-tuple-element.24) | copy-start | bytes 11796484
  118.4 18.3 %collective-permute-start.1 = (bf16[3,128,4,256]{1,3,2,0:T(8,128)(2,1)}, bf16[3,128,4,256]{1,3,2,0:T(8,128)(2,1)S(1)}, u32[]{:S(2)}, u32[]{:S(2)}) collective-permute-start(bf16[3,128,4,256]{1,3,2,0:T(8,128)(2,1)} %bitcast.34), channel_id=1, source_target_pairs={{0,2},{1,3},{2,4},{3,5},{4,6},{5,7}} | collective-permute-start | bytes 2359304 | tf_op jit(solution)/shard_map/ppermute | solution.py:91
  122.2 23.8 %collective-permute-start.2 = (bf16[3,128,4,256]{1,3,2,0:T(8,128)(2,1)}, bf16[3,128,4,256]{1,3,2,0:T(8,128)(2,1)S(1)}, u32[]{:S(2)}, u32[]{:S(2)}) collective-permute-start(bf16[3,128,4,256]{1,3,2,0:T(8,128)(2,1)} %bitcast.34), channel_id=1, source_target_pairs={{0,3},{1,4},{2,5},{3,6},{4,7}} | collective-permute-start | bytes 2359304 | tf_op jit(solution)/shard_map/ppermute | solution.py:91
  127.9 36.2 %collective-permute-start.3 = (bf16[3,128,4,256]{1,3,2,0:T(8,128)(2,1)}, bf16[3,128,4,256]{1,3,2,0:T(8,128)(2,1)S(1)}, u32[]{:S(2)}, u32[]{:S(2)}) collective-permute-start(bf16[3,128,4,256]{1,3,2,0:T(8,128)(2,1)} %bitcast.34), channel_id=1, source_target_pairs={{0,4},{1,5},{2,6},{3,7}} | collective-permute-start | bytes 2359304 | tf_op jit(solution)/shard_map/ppermute | solution.py:91
  179.8 35.2 %copy-start.2 = (bf16[3,128,2560]{2,1,0:T(8,128)(2,1)S(1)}, bf16[3,128,2560]{2,1,0:T(8,128)(2,1)}, u32[]{:S(2)}) copy-start(bf16[3,128,2560]{2,1,0:T(8,128)(2,1)} %get-tuple-element.10) | copy-start | bytes 5898244
  246.8 30.8 %copy-start.15 = (f32[2560]{0:T(1024)S(1)}, f32[2560]{0:T(1024)}, u32[]{:S(2)}) copy-start(f32[2560]{0:T(1024)} %broadcast_add_fusion.4) | copy-start | bytes 30724
  277.6 3.3 copy-start.24
  295.0 6.0 %copy-start.20 = (f32[2560]{0:T(1024)S(1)}, f32[2560]{0:T(1024)}, u32[]{:S(2)}) copy-start(f32[2560]{0:T(1024)} %param.45) | copy-start | bytes 30724
  295.0 6.1 %copy-start.21 = (f32[2560]{0:T(1024)S(1)}, f32[2560]{0:T(1024)}, u32[]{:S(2)}) copy-start(f32[2560]{0:T(1024)} %param.46) | copy-start | bytes 30724
  295.0 6.7 %copy-start.22 = (f32[2560]{0:T(1024)S(1)}, f32[2560]{0:T(1024)}, u32[]{:S(2)}) copy-start(f32[2560]{0:T(1024)} %param.47) | copy-start | bytes 30724
  295.0 7.2 %copy-start.13 = (s32[3,1024]{1,0:T(4,128)S(1)}, s32[3,1024]{1,0:T(4,128)}, u32[]{:S(2)}) copy-start(s32[3,1024]{1,0:T(4,128)} %copy-done.12) | copy-start | bytes 36868
  295.0 7.2 %copy-start.18 = (s32[3,128]{1,0:T(4,128)S(1)}, s32[3,128]{1,0:T(4,128)}, u32[]{:S(2)}) copy-start(s32[3,128]{1,0:T(4,128)} %param.25) | copy-start | bytes 4612
  295.0 8.6 %copy-start.25 = (f32[2560]{0:T(1024)S(1)}, f32[2560]{0:T(1024)}, u32[]{:S(2)}) copy-start(f32[2560]{0:T(1024)} %broadcast_add_fusion.3) | copy-start | bytes 30724
  295.0 91.1 %all-gather.3.cloned.1.call-start = ((), (), s32[]{:S(2)}) async-start(), calls=%async_computation | async-start | bytes 7077888 | tf_op jit(solution)/shard_map/all_gather | solution.py:98
  310.8 1.4 copy-start.7
  310.8 1.4 copy-start.10
  343.6 9.0 %copy-start.11 = (pred[3,128,1024]{1,2,0:T(8,128)(4,1)S(1)}, pred[3,128,1024]{1,2,0:T(8,128)(4,1)}, u32[]{:S(2)}) copy-start(pred[3,128,1024]{1,2,0:T(8,128)(4,1)} %fusion.158) | copy-start | bytes 1179652
  348.1 4.5 copy-start
  413.5 2.3 copy-start.26
  415.9 30.2 %copy-start.3 = (bf16[3,128,2560]{2,1,0:T(8,128)(2,1)S(1)}, bf16[3,128,2560]{2,1,0:T(8,128)(2,1)}, u32[]{:S(2)}) copy-start(bf16[3,128,2560]{2,1,0:T(8,128)(2,1)} %get-tuple-element.6) | copy-start | bytes 5898244
  478.0 30.3 %copy-start.14 = (f32[2560]{0:T(1024)S(1)}, f32[2560]{0:T(1024)}, u32[]{:S(2)}) copy-start(f32[2560]{0:T(1024)} %broadcast_add_fusion) | copy-start | bytes 30724
Sparse Core Ops, SparseCore 0:
  295.1 48.4 all-gather.4
  345.4 40.7 all-gather.2
where the time goes:
time: 529 us; the launch traced here: 519 us
  matrix products  271 us (51%)
  waiting for transfers between devices  78.5 us (15%)
  blocking collectives  56.1 us (11%)
  other arithmetic  42.6 us (8%)
  local copies, waits for them, and re-layouts  31.5 us (6%)
  starting transfers between devices  24.9 us (5%)
  between operations  14.5 us (3%)
    dot_general x2, matrix products, finish_layer(): jnp.einsum('btd,df->btf', normed_mid, w_gate, preferred_element_type=jnp....  65.4 us
    dot_general x2, matrix products, finish_layer(): jnp.einsum('btd,df->btf', normed_mid, w_up, preferred_element_type=jnp.fl...  63.7 us
    dot_general x2, matrix products, finish_layer(): jnp.einsum('btf,fd->btd', act_val, w_down, preferred_element_type=jnp.flo...  61.1 us
    all_gather x1, blocking collectives, device_step(): all_pos = lax.all_gather(positions, 'cp', axis=1, tiled=True)  56.1 us
    all_gather x1, waiting for transfers between devices, device_step(): key_all = lax.all_gather(key_rot, 'cp', axis=1, tiled=True)  29.3 us
    all_gather x1, waiting for transfers between devices, device_step(): value_all = lax.all_gather(value_t, 'cp', axis=1, tiled=True)  26.8 us
    dot_general x2, matrix products, attend(): jnp.einsum('bkgts,bskd->btkgd', prob_bf, value_all, preferred_element_typ...  23.3 us
    ppermute x4, waiting for transfers between devices, device_step(): value_parts.append(lax.ppermute(value_t, 'cp', perm_pairs))  22.4 us
  transfers between devices with their start and end apart: 10, of which 5 were waited for; matrix products, arithmetic and copies ran while one was open for 14% of the time, Pallas kernels for 0%

commit v1 on v0

v1 whole, which is shorter than its diff:
```python
import functools
import math

import jax
import jax.numpy as jnp
from jax import lax
from jax.experimental import pallas as pl
from jax.experimental.pallas import tpu as pltpu
from jax.sharding import PartitionSpec as P

HEAD_DIM = 256
WINDOW = 512
EPSILON = 1e-6
THETA = 10000.0
SOFT_CAP = 50.0
EXP2_CAP = SOFT_CAP * math.log2(math.e)

MESH = pl.DeviceIdType.MESH
F32 = jnp.float32
BF16 = jnp.bfloat16

ROWS = 3
TOK = 128
CTOK = 256
DIM = 2560
HQ = 1024
HKV = 512
FF = 10240
FFH = FF // 2
DH = DIM // 2
CHIPS = 4
STEPS = 2 * ROWS
DEPTH = 4
GU = FFH // 512


def dot(a, b):
    return jnp.dot(a, b, preferred_element_type=F32)


def rms(u, w):
    mean_sq = jnp.mean(u * u, axis=-1, keepdims=True)
    return (u * lax.rsqrt(mean_sq + EPSILON) * (1.0 + w)).astype(BF16)


def gated(g, u):
    g = g.astype(BF16).astype(F32)
    u = u.astype(BF16).astype(F32)
    return (jax.nn.gelu(g, approximate=True) * u).astype(BF16)


def kernel(x_hbm, tab_in, pos_in, norms,
           wq0, wk0, wv0, wo0, wg0, wu0, wd0, wq1, wk1, wv1, wo1, wg1, wu1, wd1,
           out_hbm,
           ring, kvbuf, xbuf, mbuf, hbuf, qbuf, obuf, abuf, dbuf, tab, posbuf, ebuf, gs, us,
           ring_sem, xl_sem, xs_sem, xr_sem, ts_sem, tr_sem, ps_sem, pr_sem, kvs_sem, kvr_sem,
           os_sem, or_sem, as_sem, ar_sem, hs_sem, hr_sem, dss_sem, dr_sem, out_sem):
    me = lax.axis_index("cp")
    chip = me // 2
    core = me % 2
    peer = me + 1 - 2 * core

    def at(dev):
        return {"cp": dev}

    def start_cols(w, rows, col, slot, row0):
        pltpu.make_async_copy(
            w.at[pl.ds(0, rows), pl.ds(pl.multiple_of(col, 256), 256)],
            ring.at[slot, pl.ds(row0, rows), :], ring_sem.at[slot]).start()

    def by_layer(first, f0, f1):
        @pl.when(first)
        def _():
            f0()

        @pl.when(jnp.logical_not(first))
        def _():
            f1()

    def start_gu(first, i, slot):
        def go(wg, wu):
            col = core * FFH + i * 512
            for t in range(2):
                start_cols(wg, DIM, col + 256 * t, slot, 2 * t * DIM)
                start_cols(wu, DIM, col + 256 * t, slot, (2 * t + 1) * DIM)
        by_layer(first, lambda: go(wg0, wu0), lambda: go(wg1, wu1))

    def start_down(first, n, slot):
        def go(wd):
            start_cols(wd, FF, core * DH + n * 256, slot, 0)
        by_layer(first, lambda: go(wd0), lambda: go(wd1))

    def start_wo(first, slot):
        def go(wo):
            for t in range(5):
                start_cols(wo, 2048, core * DH + t * 256, slot, t * 2048)
        by_layer(first, lambda: go(wo0), lambda: go(wo1))

    def start_kv(wk, wv, slot):
        for t in range(2):
            start_cols(wk, DIM, core * HKV + t * 256, slot, t * DIM)
            start_cols(wv, DIM, core * HKV + t * 256, slot, (2 + t) * DIM)

    def start_q(wq, slot):
        for t in range(4):
            start_cols(wq, DIM, core * HQ + t * 256, slot, t * DIM)

    def wait_w(slot):
        pltpu.make_async_copy(wd0.at[:, pl.ds(0, 256)], ring.at[slot], ring_sem.at[slot]).wait()

    def unit(slot, t, rows=DIM):
        return ring[slot, pl.ds(t * rows, rows), :]

    def x_local(r):
        return pltpu.make_async_copy(
            x_hbm.at[r], xbuf.at[r, pl.ds(pl.multiple_of(core * TOK, TOK), TOK), :], xl_sem.at[r])

    def x_remote(r):
        return pltpu.make_async_remote_copy(
            x_hbm.at[r], xbuf.at[r, pl.ds(pl.multiple_of(core * TOK, TOK), TOK), :],
            xs_sem.at[r], xr_sem.at[r], device_id=at(peer), device_id_type=MESH)

    def tab_local():
        return pltpu.make_async_copy(tab_in, tab.at[core], ts_sem.at[0])

    def tab_remote():
        return pltpu.make_async_remote_copy(
            tab_in, tab.at[core], ts_sem.at[1], tr_sem.at[0], device_id=at(peer), device_id_type=MESH)

    def pos_local():
        return pltpu.make_async_copy(pos_in, posbuf.at[me], ps_sem.at[0])

    def pos_remote(k):
        return pltpu.make_async_remote_copy(
            pos_in, posbuf.at[me], ps_sem.at[k], pr_sem.at[k],
            device_id=at(lax.rem(me + k, 8)), device_id_type=MESH)

    def kv_remote(l, r, d):
        return pltpu.make_async_remote_copy(
            kvbuf.at[l, r, chip], kvbuf.at[l, r, chip], kvs_sem.at[l, r, d], kvr_sem.at[l, r, d],
            device_id=at(lax.rem(me + 2 * d, 8)), device_id_type=MESH)

    def half(buf, width):
        return buf.at[:, pl.ds(pl.multiple_of(core * width, 256), width)]

    def o_remote():
        return pltpu.make_async_remote_copy(
            half(obuf, HQ), half(obuf, HQ), os_sem, or_sem, device_id=at(peer), device_id_type=MESH)

    def a_remote():
        return pltpu.make_async_remote_copy(
            half(abuf, DH), half(abuf, DH), as_sem, ar_sem, device_id=at(peer), device_id_type=MESH)

    def d_remote(par):
        return pltpu.make_async_remote_copy(
            half(dbuf.at[par], DH), half(dbuf.at[par], DH), dss_sem.at[par], dr_sem.at[par],
            device_id=at(peer), device_id_type=MESH)

    def h_remote(par, i):
        w = hbuf.at[par, :, pl.ds(pl.multiple_of(core * FFH + i * 512, 512), 512)]
        return pltpu.make_async_remote_copy(
            w, w, hs_sem.at[par], hr_sem.at[par], device_id=at(peer), device_id_type=MESH)

    def h_all(par):
        w = hbuf.at[par, :, pl.ds(pl.multiple_of(core * FFH, 512), FFH)]
        return pltpu.make_async_remote_copy(
            w, w, hs_sem.at[par], hr_sem.at[par], device_id=at(peer), device_id_type=MESH)

    def rope(y, r, t, dst):
        y = y.astype(BF16).astype(F32)
        for c in range(2):
            f = y[c * TOK:(c + 1) * TOK, :128]
            s = y[c * TOK:(c + 1) * TOK, 128:]
            cos = tab[c, r, 0]
            sin = tab[c, r, 1]
            dst(c, (f * cos - s * sin) * t, (s * cos + f * sin) * t)

    def kv_part(src, slot, l, r):
        for t in range(2):
            y = dot(src(), unit(slot, t))

            def put(c, a, b, t=t):
                rows = pl.ds(c * TOK, TOK)
                kvbuf[l, r, chip, rows, t * 256:t * 256 + 128] = a.astype(BF16)
                kvbuf[l, r, chip, rows, t * 256 + 128:t * 256 + 256] = b.astype(BF16)
            rope(y, r, 1.0, put)
            kvbuf[l, r, chip, :, HKV + t * 256:HKV + t * 256 + 256] = dot(src(), unit(slot, 2 + t)).astype(BF16)

    def q_part(src, slot, r):
        for t in range(4):
            y = dot(src(), unit(slot, t))

            def put(c, a, b, t=t):
                rows = pl.ds(c * TOK, TOK)
                qbuf[r, t, rows, 0:128] = a.astype(BF16)
                qbuf[r, t, rows, 128:256] = b.astype(BF16)
            rope(y, r, HEAD_DIM ** -0.5, put)

    def send_kv(l, r, far):
        for d in range(1, far + 1):
            @pl.when(chip + d < CHIPS)
            def _(d=d):
                kv_remote(l, r, d).start()

    def attention(j):
        l = j // ROWS
        r = j % ROWS
        for d in range(1, CHIPS):
            @pl.when((chip - d >= 0) & (d <= 2 + l))
            def _(d=d):
                kv_remote(l, r, d).wait_recv()
        lo = jnp.where(l == 1, 0, jnp.maximum(chip - 2, 0))
        count = chip - lo + 1
        reach = WINDOW + l * 1000000

        def kv_head(kh, carry):
            kcol = pl.multiple_of(kh * 256, 256)
            vcol = pl.multiple_of(HKV + kh * 256, 256)

            def score(t, sums):
                b = lo + t
                k = kvbuf[l, r, b, :, pl.ds(kcol, 256)]
                new = []
                masks = []
                for c in range(2):
                    qp = tab[c, r, 2]
                    parts = []
                    for kc in range(2):
                        off = qp - posbuf[2 * b + kc, pl.ds(r, 1), :]
                        parts.append((off >= 0.0) & (off < reach.astype(F32)))
                    masks.append(parts)
                for hh in range(2):
                    q = qbuf[r, 2 * kh + hh]
                    s = lax.dot_general(q, k, (((1,), (1,)), ((), ())), preferred_element_type=F32)
                    e = jnp.exp2(EXP2_CAP * jnp.tanh(s * (1.0 / SOFT_CAP)))
                    out = []
                    for c in range(2):
                        tot = None
                        for kc in range(2):
                            piece = jnp.where(masks[c][kc], e[c * TOK:(c + 1) * TOK, kc * 128:(kc + 1) * 128], 0.0)
                            ebuf[hh, t, c * TOK:(c + 1) * TOK, kc * 128:(kc + 1) * 128] = piece
                            tot = piece if tot is None else tot + piece
                        out.append(tot)
                    new.append(sums[hh] + jnp.concatenate(out, axis=0))
                return tuple(new)

            zero = jnp.zeros((CTOK, 128), F32)
            sums = lax.fori_loop(0, count, score, (zero, zero))
            inv = [1.0 / jnp.sum(s, axis=-1, keepdims=True) for s in sums]

            def mix(t, accs):
                v = kvbuf[l, r, lo + t, :, pl.ds(vcol, 256)]
                return tuple(accs[hh] + dot((ebuf[hh, t] * inv[hh]).astype(BF16), v) for hh in range(2))

            z2 = jnp.zeros((CTOK, HEAD_DIM), F32)
            accs = lax.fori_loop(0, count, mix, (z2, z2))
            for hh in range(2):
                col = pl.multiple_of(core * HQ + (2 * kh + hh) * 256, 256)
                obuf[:, pl.ds(col, 256)] = accs[hh].astype(BF16)
            return carry

        lax.fori_loop(0, 2, kv_head, 0)
        o_remote().start()

    def out_proj(slot):
        o_remote().wait()
        wait_w(slot)
        for t in range(5):
            col = pl.multiple_of(core * DH + t * 256, 256)
            abuf[:, pl.ds(col, 256)] = dot(obuf[...], unit(slot, t, 2048)).astype(BF16)
        a_remote().start()

    def mid_norm(j):
        l = j // ROWS
        r = j % ROWS
        a_remote().wait()

        def chunk(i, carry):
            rows = pl.ds(pl.multiple_of(i * 16, 16), 16)
            y = rms(abuf[rows, :].astype(F32), norms[pl.ds(4 * l + 1, 1), :])
            x1 = (xbuf[r, rows, :].astype(F32) + y.astype(F32)).astype(BF16)
            xbuf[r, rows, :] = x1
            mbuf[rows, :] = rms(x1.astype(F32), norms[pl.ds(4 * l + 2, 1), :])
            return carry
        lax.fori_loop(0, CTOK // 16, chunk, 0)

    def end_norm(j, par):
        l = j // ROWS
        r = j % ROWS
        d_remote(par).wait()

        def chunk(i, carry):
            rows = pl.ds(pl.multiple_of(i * 16, 16), 16)
            y = rms(dbuf[par, rows, :].astype(F32), norms[pl.ds(4 * l + 3, 1), :])
            x2 = (xbuf[r, rows, :].astype(F32) + y.astype(F32)).astype(BF16)
            xbuf[r, rows, :] = x2
            mbuf[rows, :] = rms(x2.astype(F32), norms[4:5, :])
            return carry
        lax.fori_loop(0, CTOK // 16, chunk, 0)

    def put_out(j):
        r = j % ROWS
        return pltpu.make_async_copy(
            xbuf.at[r, pl.ds(pl.multiple_of(core * TOK, TOK), TOK), :], out_hbm.at[r], out_sem.at[r])

    start_kv(wk0, wv0, 0)
    start_q(wq0, 1)
    start_wo(me >= 0, 2)
    for r in range(ROWS):
        x_local(r).start()
    tab_local().start()
    pos_local().start()
    barrier = pltpu.get_barrier_semaphore()
    for k in range(1, 8):
        pl.semaphore_signal(barrier, inc=1, device_id=at(lax.rem(me + k, 8)), device_id_type=MESH)
    pl.semaphore_wait(barrier, 7)
    x_remote(0).start()
    tab_remote().start()
    for r in range(1, ROWS):
        x_remote(r).start()
    for k in range(1, 8):
        pos_remote(k).start()

    def first_norm(r, carry):
        x_local(r).wait()
        x_remote(r).wait()

        def chunk(i, carry):
            rows = pl.ds(pl.multiple_of(i * 16, 16), 16)
            hbuf[0, rows, pl.ds(pl.multiple_of(r * DIM, DIM), DIM)] = rms(
                xbuf[r, rows, :].astype(F32), norms[0:1, :])
            return carry
        lax.fori_loop(0, CTOK // 16, chunk, 0)
        return carry

    start_gu(me >= 0, 0, 3)
    tab_local().wait()
    tab_remote().wait()
    wait_w(0)

    def a0(r):
        return hbuf[0, :, pl.ds(pl.multiple_of(r * DIM, DIM), DIM)]

    def first_kv(r, carry):
        first_norm(r, 0)
        kv_part(lambda: a0(r), 0, 0, r)
        send_kv(0, r, 2)
        return carry
    lax.fori_loop(0, ROWS, first_kv, 0)
    start_gu(me >= 0, 1, 0)
    wait_w(1)

    def first_q(r, carry):
        q_part(lambda: a0(r), 1, r)
        return carry
    lax.fori_loop(0, ROWS, first_q, 0)
    pos_local().wait()
    for k in range(1, 8):
        pos_remote(k).wait()
    start_gu(me >= 0, 2, 1)
    attention(0 * me)
    out_proj(2)

    def step(j, carry):
        first = j < ROWS
        first_next = j + 1 < ROWS
        par = j % 2
        has_qkv = (j >= 1) & (j <= ROWS)
        extra = jnp.where(has_qkv, 2, 0)
        done = jnp.where(j >= 1, jnp.minimum(j - 1, ROWS), 0)
        cb = 3 + 2 * done
        db = cb + GU + extra

        def sl(p):
            return lax.rem(p, DEPTH)

        mid_norm(j)

        def gate_up(i, carry):
            @pl.when(i + 3 < GU)
            def _():
                start_gu(first, i + 3, sl(cb + i + 3))

            @pl.when(i + 3 >= GU)
            def _():
                e = i + 3 - GU

                @pl.when(jnp.logical_not(has_qkv))
                def _():
                    start_down(first, e, sl(cb + i + 3))

                @pl.when(has_qkv & (e == 0))
                def _():
                    start_kv(wk1, wv1, sl(cb + i + 3))

                @pl.when(has_qkv & (e == 1))
                def _():
                    start_q(wq1, sl(cb + i + 3))

                @pl.when(has_qkv & (e == 2))
                def _():
                    start_down(first, 0, sl(cb + i + 3))

            @pl.when(i >= 2)
            def _():
                h_remote(par, i - 2).start()
            slot = sl(cb + i)
            wait_w(slot)
            base = core * FFH + i * 512
            prev = jnp.where(i >= 1, base - 256, base + 256)
            hbuf[par, :, pl.ds(pl.multiple_of(prev, 256), 256)] = gated(gs[...], us[...])
            g = dot(mbuf[...], unit(slot, 0))
            u = dot(mbuf[...], unit(slot, 1))
            hbuf[par, :, pl.ds(pl.multiple_of(base, 256), 256)] = gated(g, u)
            gs[...] = dot(mbuf[...], unit(slot, 2))
            us[...] = dot(mbuf[...], unit(slot, 3))
            return carry
        lax.fori_loop(0, GU, gate_up, 0)
        last = core * FFH + FFH - 256
        hbuf[par, :, pl.ds(pl.multiple_of(last, 256), 256)] = gated(gs[...], us[...])
        h_remote(par, GU - 2).start()
        h_remote(par, GU - 1).start()

        @pl.when(j >= 1)
        def _():
            end_norm(j - 1, 1 - par)

            @pl.when(has_qkv)
            def _():
                r = j - 1
                start_down(first, 1, sl(db + 1))
                wait_w(sl(cb + GU))
                kv_part(lambda: mbuf[...], sl(cb + GU), 1, r)
                send_kv(1, r, 3)
                start_down(first, 2, sl(db + 2))
                wait_w(sl(cb + GU + 1))
                q_part(lambda: mbuf[...], sl(cb + GU + 1), r)

            @pl.when(jnp.logical_not(has_qkv))
            def _():
                put_out(j - 1).start()

        @pl.when(j + 1 < STEPS)
        def _():
            attention(j + 1)

        h_all(par).wait()

        def down(n, pos):
            wait_w(sl(pos))
            col = pl.multiple_of(core * DH + n * 256, 256)
            y = dot(hbuf[par, :, 0:FFH], ring[sl(pos), 0:FFH, :]) + dot(hbuf[par, :, FFH:FF], ring[sl(pos), FFH:FF, :])
            dbuf[par, :, pl.ds(col, 256)] = y.astype(BF16)

        def down_a(n, carry):
            @pl.when(j + 1 < STEPS)
            def _():
                @pl.when(n == 0)
                def _():
                    start_wo(first_next, sl(db + 3))

                @pl.when(n >= 1)
                def _():
                    start_down(first, n + 2, sl(db + n + 3))

            @pl.when((j + 1 == STEPS) & (n <= 1))
            def _():
                start_down(first, n + 3, sl(db + n + 3))
            down(n, db + n)
            return carry
        lax.fori_loop(0, 3, down_a, 0)

        @pl.when(j + 1 < STEPS)
        def _():
            start_gu(first_next, 0, sl(db + 6))
            out_proj(sl(db + 3))

        shift = jnp.where(j + 1 < STEPS, 1, 0)

        def down_b(n, carry):
            @pl.when(j + 1 < STEPS)
            def _():
                start_gu(first_next, n - 2, sl(db + n + 4))
            down(n, db + n + shift)
            return carry
        lax.fori_loop(3, 5, down_b, 0)
        d_remote(par).start()
        return carry

    lax.fori_loop(0, STEPS, step, 0)

    end_norm(STEPS - 1 + 0 * me, (STEPS - 1) % 2)
    put_out(STEPS - 1).start()
    for r in range(ROWS):
        put_out(r).wait()
    for l in range(2):
        for r in range(ROWS):
            for d in range(1, 3 + l):
                @pl.when(chip + d < CHIPS)
                def _(l=l, r=r, d=d):
                    kv_remote(l, r, d).wait_send()


def solution(mesh):
    def device_step(hidden, positions, *weights):
        local_w = weights[:11]
        global_w = weights[11:]
        half_dim = HEAD_DIM // 2
        inv_freq = THETA ** (-(jnp.arange(half_dim, dtype=F32) * 2.0 / HEAD_DIM))
        pos = positions.astype(F32)
        angles = pos[:, :, None] * inv_freq
        tab = jnp.stack([jnp.cos(angles), jnp.sin(angles), jnp.broadcast_to(pos[:, :, None], angles.shape)], axis=1)
        pos_rows = jnp.pad(pos, ((0, 8 - ROWS), (0, 0)))
        norms = jnp.stack(local_w[7:11] + global_w[7:11])
        hbm = pl.BlockSpec(memory_space=pltpu.HBM)
        vmem = pl.BlockSpec(memory_space=pltpu.VMEM)
        dma = pltpu.SemaphoreType.DMA
        flops = 2 * ROWS * TOK * 2 * (DIM * 4096 + 2048 * DIM + 3 * DIM * FF)
        return pl.pallas_call(
            kernel,
            out_shape=jax.ShapeDtypeStruct(hidden.shape, hidden.dtype),
            in_specs=[hbm, vmem, vmem, vmem] + [hbm] * 14,
            out_specs=hbm,
            scratch_shapes=[
                pltpu.VMEM((DEPTH, FF, 256), BF16),
                pltpu.VMEM((2, ROWS, CHIPS, CTOK, 2 * HKV), BF16),
                pltpu.VMEM((ROWS, CTOK, DIM), BF16),
                pltpu.VMEM((CTOK, DIM), BF16),
                pltpu.VMEM((2, CTOK, FF), BF16),
                pltpu.VMEM((ROWS, 4, CTOK, HEAD_DIM), BF16),
                pltpu.VMEM((CTOK, 2 * HQ), BF16),
                pltpu.VMEM((CTOK, DIM), BF16),
                pltpu.VMEM((2, CTOK, DIM), BF16),
                pltpu.VMEM((2, ROWS, 3, TOK, 128), F32),
                pltpu.VMEM((8, 8, 128), F32),
                pltpu.VMEM((2, CHIPS, CTOK, CTOK), F32),
                pltpu.VMEM((CTOK, 256), F32),
                pltpu.VMEM((CTOK, 256), F32),
                dma((DEPTH,)), dma((ROWS,)), dma((ROWS,)), dma((ROWS,)),
                dma((2,)), dma((1,)), dma((8,)), dma((8,)),
                dma((2, ROWS, CHIPS)), dma((2, ROWS, CHIPS)),
                dma, dma, dma, dma,
                dma((2,)), dma((2,)), dma((2,)), dma((2,)), dma((ROWS,)),
            ],
            compiler_params=pltpu.CompilerParams(
                collective_id=0, has_side_effects=True, vmem_limit_bytes=67043328),
            cost_estimate=pl.CostEstimate(flops=flops, bytes_accessed=600000000, transcendentals=0),
            name="layers",
        )(hidden, tab, pos_rows, norms, *local_w[:7], *global_w[:7])

    specs_in = tuple([P("dp", "cp"), P("dp", "cp")] + [P()] * 22)
    return jax.shard_map(device_step, mesh=mesh, in_specs=specs_in, out_specs=P("dp", "cp"), check_vma=False)
```

time: 529 us -> 313 us (0.59)
  the two profiles are of different devices: /device:TPU:0 before, /device:TPU:5 now
where the time goes in v1:
time: 313 us; the launch traced here: 312 us
  Pallas kernels  300 us (96%)
  local copies, waits for them, and re-layouts  10.1 us (3%)
    pallas_call x1, Pallas kernels, device_step(): pl.pallas_call(kernel, out_shape=jax.ShapeDtypeStruct(hidden.shape, hidde...  300 us
    another operation x9, local copies, waits for them, and re-layouts, device_step(): norms = jnp.stack(local_w[7:11] + global_w[7:11])  6.46 us

profile of v1, /device:TPU:5, one launch (start us, length us, event | category | flops | bytes accessed | tf_op | source)
XLA Modules:
  0.0 312.0 jit_solution(5359983069870334210)
XLA Ops:
  0.0 0.7 convert_element_type.5
  0.7 0.6 pad.4.pos_in
  1.3 0.7 stack.33
  2.0 0.7 stack.34
  2.7 0.7 stack.35
  3.4 0.7 stack.36
  4.2 0.7 stack.37
  4.9 0.7 stack.38
  5.6 0.7 stack.39
  6.3 0.7 stack.40
  7.0 0.8 stack.41.norms
  7.8 0.1 mul.27
  7.9 0.8 multiply_cosine_fusion
  8.6 0.9 pad_maximum_fusion.tab_in
  9.5 299.6 %layers.1 = bf16[3,128,2560]{2,1,0:T(8,128)(2,1)} custom-call(bf16[3,128,2560]{2,1,0:T(8,128)(2,1)} %x_hbm.1, f32[3,3,128,128]{3,2,1,0:T(8,128)} %pad_maximum_fusion.tab_in, f32[8,128]{1,0:T(8,128)} %pad.4.pos_in, f32[8,2560]{1,0:T(8,128)} %stack.41.norms, bf16[2560,2048]{1,0:T(8,128)(2,1)} %wq0.1, bf16[2560,1024]{1,0:T(8,128)(2,1)} %wk0.1, ...), custom_call_target="tpu_custom_call" | custom-call | flops 144955146240 | bytes 600000000 | tf_op jit(solution)/shard_map/layers/pallas_call | solution.py:519
  309.1 2.9 copy.26
  (1 shorter events, 0.0 us)

commit v2 on v1

v2 whole, which is shorter than its diff:
```python
import functools
import math

import jax
import jax.numpy as jnp
import numpy as np
from jax import lax
from jax.experimental import pallas as pl
from jax.experimental.pallas import tpu as pltpu
from jax.sharding import PartitionSpec as P

HEAD_DIM = 256
WINDOW = 512
EPSILON = 1e-6
THETA = 10000.0
SOFT_CAP = 50.0
EXP2_CAP = SOFT_CAP * math.log2(math.e)

MESH = pl.DeviceIdType.MESH
F32 = jnp.float32
BF16 = jnp.bfloat16

ROWS = 3
TOK = 128
CTOK = 256
DIM = 2560
HQ = 1024
HKV = 512
FF = 10240
FFH = FF // 2
DH = DIM // 2
CHIPS = 4
STEPS = 2 * ROWS
DEPTH = 4
GU = FFH // 512
SCORES = 8
NCHUNK = 128
PIECE = 16
KEYS = CHIPS * CTOK


def dot(a, b):
    return jnp.dot(a, b, preferred_element_type=F32)


def rms(u, w):
    mean_sq = jnp.mean(u * u, axis=-1, keepdims=True)
    return (u * lax.rsqrt(mean_sq + EPSILON) * (1.0 + w)).astype(BF16)


def gated(g, u):
    g = g.astype(BF16).astype(F32)
    u = u.astype(BF16).astype(F32)
    return (jax.nn.gelu(g, approximate=True) * u).astype(BF16)


def kernel(x_hbm, pos_in, freq_in, n0, n1, n2, n3, n4, n5, n6, n7,
           wq0, wk0, wv0, wo0, wg0, wu0, wd0, wq1, wk1, wv1, wo1, wg1, wu1, wd1,
           out_hbm,
           ring, kvbuf, xbuf, mbuf, hown, hpeer, qbuf, obuf, abuf, dbuf, cosb, sinb, tposb, posbuf, freq, norms, r0, r1, r2, r3, r4, r5, r6, r7, ebuf, sbuf, gs, us, gb, ub,
           n_sem, ring_sem, xl_sem, xs_sem, xr_sem, ps_sem, pr_sem, kvs_sem, kvr_sem, ks_sem, kr_sem,
           os_sem, or_sem, as_sem, ar_sem, hs_sem, hr_sem, dss_sem, dr_sem, out_sem):
    me = lax.axis_index("cp")
    chip = me // 2
    core = me % 2
    peer = me + 1 - 2 * core

    def at(dev):
        return {"cp": dev}

    def start_cols(w, rows, col, slot, row0):
        pltpu.make_async_copy(
            w.at[pl.ds(0, rows), pl.ds(pl.multiple_of(col, 256), 256)],
            ring.at[slot, pl.ds(row0, rows), :], ring_sem.at[slot]).start()

    def by_layer(first, f0, f1):
        @pl.when(first)
        def _():
            f0()

        @pl.when(jnp.logical_not(first))
        def _():
            f1()

    def start_gu(first, i, slot):
        def go(wg, wu):
            col = core * FFH + i * 512
            for t in range(2):
                start_cols(wg, DIM, col + 256 * t, slot, 2 * t * DIM)
                start_cols(wu, DIM, col + 256 * t, slot, (2 * t + 1) * DIM)
        by_layer(first, lambda: go(wg0, wu0), lambda: go(wg1, wu1))

    def start_down(first, n, slot):
        def go(wd):
            start_cols(wd, FF, core * DH + n * 256, slot, 0)
        by_layer(first, lambda: go(wd0), lambda: go(wd1))

    def start_wo(first, slot):
        def go(wo):
            for t in range(5):
                start_cols(wo, 2048, core * DH + t * 256, slot, t * 2048)
        by_layer(first, lambda: go(wo0), lambda: go(wo1))

    def start_kv(wk, wv, slot):
        for t in range(2):
            start_cols(wk, DIM, core * HKV + t * 256, slot, t * DIM)
            start_cols(wv, DIM, core * HKV + t * 256, slot, (2 + t) * DIM)

    def start_q(wq, slot):
        for t in range(4):
            start_cols(wq, DIM, core * HQ + t * 256, slot, t * DIM)

    def wait_w(slot):
        pltpu.make_async_copy(wd0.at[:, pl.ds(0, 256)], ring.at[slot], ring_sem.at[slot]).wait()

    def unit(slot, t, rows=DIM):
        return ring[slot, pl.ds(t * rows, rows), :]

    def x_local(r):
        return pltpu.make_async_copy(
            x_hbm.at[r], xbuf.at[r, pl.ds(pl.multiple_of(core * TOK, TOK), TOK), :], xl_sem.at[r])

    def x_remote(r):
        return pltpu.make_async_remote_copy(
            x_hbm.at[r], xbuf.at[r, pl.ds(pl.multiple_of(core * TOK, TOK), TOK), :],
            xs_sem.at[r], xr_sem.at[r], device_id=at(peer), device_id_type=MESH)

    def norm_copy(k, src):
        return pltpu.make_async_copy(src, nraw[k], n_sem.at[k])

    all_norms = (n0, n1, n2, n3, n4, n5, n6, n7)
    nraw = (r0, r1, r2, r3, r4, r5, r6, r7)

    def freq_copy():
        return pltpu.make_async_copy(freq_in, freq, n_sem.at[8])

    def tables(c):
        rows = posbuf[2 * chip + c].astype(F32)
        cols = jnp.transpose(jnp.concatenate([rows, jnp.zeros((TOK - ROWS, TOK), F32)], axis=0))
        for r in range(ROWS):
            col = jnp.broadcast_to(cols[:, r:r + 1], (TOK, 128))
            tposb[c, r] = col.astype(jnp.int32)
            angle = col * freq[...]
            cosb[c, r] = jnp.cos(angle)
            sinb[c, r] = jnp.sin(angle)

    def pos_local():
        return pltpu.make_async_copy(pos_in, posbuf.at[me], ps_sem.at[0])

    def pos_remote(k):
        return pltpu.make_async_remote_copy(
            pos_in, posbuf.at[me], ps_sem.at[k], pr_sem.at[k],
            device_id=at(lax.rem(me + k, 8)), device_id_type=MESH)

    def kv_own(l, r):
        return kvbuf.at[l, r, pl.ds(pl.multiple_of(chip * CTOK, CTOK), CTOK), :]

    def kv_remote(l, r, d):
        return pltpu.make_async_remote_copy(
            kv_own(l, r), kv_own(l, r), kvs_sem.at[l, r, d], kvr_sem.at[l, r, d],
            device_id=at(lax.rem(me + 2 * d, 8)), device_id_type=MESH)

    def kv_piece(r, h):
        return kvbuf.at[0, r, pl.ds(pl.multiple_of(CTOK + h * TOK, TOK), TOK), :]

    def kv_second(r, h):
        return pltpu.make_async_remote_copy(
            kv_piece(r, h), kv_piece(r, h), ks_sem.at[r, h], kr_sem.at[r, h],
            device_id=at(6 + core), device_id_type=MESH)

    def kv_relay(r, h):
        return pltpu.make_async_remote_copy(
            kv_piece(r, h), kv_piece(r, h), ks_sem.at[r, h], kr_sem.at[r, h],
            device_id=at(4 + core), device_id_type=MESH)

    def forward(r, h):
        @pl.when(chip == 3)
        def _():
            kv_second(r, h).wait_recv()
            kv_relay(r, h).start()

    def send_kv0(r):
        @pl.when(chip == 0)
        def _():
            kv_remote(0, r, 2).start()
            kv_remote(0, r, 1).start()

        @pl.when(chip == 1)
        def _():
            for h in range(2):
                kv_second(r, h).start()

        @pl.when(chip == 2)
        def _():
            kv_remote(0, r, 1).start()

    def half(buf, width):
        return buf.at[:, pl.ds(pl.multiple_of(core * width, 256), width)]

    def o_remote():
        return pltpu.make_async_remote_copy(
            half(obuf, HQ), half(obuf, HQ), os_sem, or_sem, device_id=at(peer), device_id_type=MESH)

    def a_remote():
        return pltpu.make_async_remote_copy(
            half(abuf, DH), half(abuf, DH), as_sem, ar_sem, device_id=at(peer), device_id_type=MESH)

    def d_remote(par):
        return pltpu.make_async_remote_copy(
            half(dbuf.at[par], DH), half(dbuf.at[par], DH), dss_sem.at[par], dr_sem.at[par],
            device_id=at(peer), device_id_type=MESH)

    def h_remote(par, i):
        cols = pl.ds(pl.multiple_of(i * 512, 512), 512)
        return pltpu.make_async_remote_copy(
            hown.at[:, cols], hpeer.at[par, :, cols], hs_sem.at[par], hr_sem.at[par],
            device_id=at(peer), device_id_type=MESH)

    def h_all(par):
        return pltpu.make_async_remote_copy(
            hown, hpeer.at[par], hs_sem.at[par], hr_sem.at[par], device_id=at(peer), device_id_type=MESH)

    def rope(y, r, t, dst):
        y = y.astype(BF16).astype(F32)
        for c in range(2):
            f = y[c * TOK:(c + 1) * TOK, :128]
            s = y[c * TOK:(c + 1) * TOK, 128:]
            cos = cosb[c, r]
            sin = sinb[c, r]
            dst(c, (f * cos - s * sin) * t, (s * cos + f * sin) * t)

    def kv_part(src, slot, l, r):
        for t in range(2):
            y = dot(src(), unit(slot, t))

            def put(c, a, b, t=t):
                rows = pl.ds(pl.multiple_of(chip * CTOK + c * TOK, TOK), TOK)
                kvbuf[l, r, rows, t * 256:t * 256 + 128] = a.astype(BF16)
                kvbuf[l, r, rows, t * 256 + 128:t * 256 + 256] = b.astype(BF16)
            rope(y, r, 1.0, put)
            kvbuf[l, r, pl.ds(pl.multiple_of(chip * CTOK, CTOK), CTOK), HKV + t * 256:HKV + t * 256 + 256] = dot(src(), unit(slot, 2 + t)).astype(BF16)

    def q_part(src, slot, r):
        for t in range(4):
            y = dot(src(), unit(slot, t))

            def put(c, a, b, t=t):
                rows = pl.ds(c * TOK, TOK)
                qbuf[r, t, rows, 0:128] = a.astype(BF16)
                qbuf[r, t, rows, 128:256] = b.astype(BF16)
            rope(y, r, HEAD_DIM ** -0.5, put)

    def send_kv(l, r, far):
        for d in range(1, far + 1):
            @pl.when(chip + d < CHIPS)
            def _(d=d):
                kv_remote(l, r, d).start()

    def kv_wait(j):
        l = j // ROWS
        r = j % ROWS
        for d in range(1, CHIPS):
            @pl.when((chip - d >= 0) & (l == 1))
            def _(d=d):
                kv_remote(1, r, d).wait_recv()

        @pl.when(l == 0)
        def _():
            @pl.when((chip == 1) | (chip == 3))
            def _():
                kv_remote(0, r, 1).wait_recv()

            @pl.when(chip == 2)
            def _():
                kv_remote(0, r, 2).wait_recv()
                for h in range(2):
                    kv_relay(r, h).wait_recv()

    def score(j, kh, t):
        l = j // ROWS
        r = j % ROWS
        reach = WINDOW + l * 1000000
        k = kvbuf[l, r, pl.ds(pl.multiple_of(t * CTOK, CTOK), CTOK), pl.ds(pl.multiple_of(kh * 256, 256), 256)]
        masks = {}
        for c in range(2):
            for kc in range(2):
                off = tposb[c, r] - posbuf[2 * t + kc, pl.ds(r, 1), :]
                masks[c, kc] = (off >= 0) & (off < reach)
        for hh in range(2):
            q = qbuf[r, 2 * kh + hh]
            s = lax.dot_general(q, k, (((1,), (1,)), ((), ())), preferred_element_type=F32)
            e = jnp.exp2(EXP2_CAP * jnp.tanh(s * (1.0 / SOFT_CAP)))
            for c in range(2):
                rows = slice(c * TOK, (c + 1) * TOK)
                tot = jnp.where(t == 0, 0.0, sbuf[2 * kh + hh, rows, :])
                for kc in range(2):
                    piece = jnp.where(masks[c, kc], e[rows, kc * 128:(kc + 1) * 128], 0.0)
                    ebuf[2 * kh + hh, rows, pl.ds(pl.multiple_of(t * CTOK + kc * 128, 128), 128)] = piece
                    tot = tot + piece
                sbuf[2 * kh + hh, rows, :] = tot

    def mix(j, kh):
        l = j // ROWS
        r = j % ROWS
        v = kvbuf[l, r, :, pl.ds(pl.multiple_of(HKV + kh * 256, 256), 256)]
        for hh in range(2):
            inv = 1.0 / jnp.sum(sbuf[2 * kh + hh], axis=-1, keepdims=True)
            p = (ebuf[2 * kh + hh] * inv).astype(BF16)
            col = pl.multiple_of(core * HQ + (2 * kh + hh) * 256, 256)
            obuf[:, pl.ds(col, 256)] = dot(p, v).astype(BF16)

    def attention(j):
        with jax.named_scope("att_wait"):
            forward(0, 1)
            kv_wait(j)
        with jax.named_scope("att"):
            def go(i, carry):
                score(j, i // CHIPS, i % CHIPS)
                return carry
            lax.fori_loop(0, SCORES, go, 0)

            def go2(i, carry):
                mix(j, i)
                return carry
            lax.fori_loop(0, 2, go2, 0)
        o_remote().start()

    def out_proj(slot):
        with jax.named_scope("o_wait"):
            o_remote().wait()
        with jax.named_scope("wo_wait"):
            wait_w(slot)
        for t in range(5):
            col = pl.multiple_of(core * DH + t * 256, 256)
            abuf[:, pl.ds(col, 256)] = dot(obuf[...], unit(slot, t, 2048)).astype(BF16)
        a_remote().start()

    def mid_rows(j, base, keep=None):
        l = j // ROWS
        r = j % ROWS
        for t in range(0, NCHUNK, PIECE):
            rows = pl.ds(pl.multiple_of(base + t, PIECE), PIECE)
            y = rms(abuf[rows, :].astype(F32), norms[4 * l + 1])
            x = xbuf[r, rows, :]
            x1 = (x.astype(F32) + y.astype(F32)).astype(BF16)
            xbuf[r, rows, :] = x1 if keep is None else jnp.where(keep, x1, x)
            mbuf[rows, :] = rms(x1.astype(F32), norms[4 * l + 2])

    def end_rows(j, par, base, keep=None):
        l = j // ROWS
        r = j % ROWS
        for t in range(0, NCHUNK, PIECE):
            rows = pl.ds(pl.multiple_of(base + t, PIECE), PIECE)
            y = rms(dbuf[par, rows, :].astype(F32), norms[4 * l + 3])
            x = xbuf[r, rows, :]
            x2 = (x.astype(F32) + y.astype(F32)).astype(BF16)
            xbuf[r, rows, :] = x2 if keep is None else jnp.where(keep, x2, x)
            dbuf[par, rows, :] = rms(x2.astype(F32), norms[4])

    def put_out(j):
        r = j % ROWS
        return pltpu.make_async_copy(
            xbuf.at[r, pl.ds(pl.multiple_of(core * TOK, TOK), TOK), :], out_hbm.at[r], out_sem.at[r])

    pos_local().start()
    x_local(0).start()
    freq_copy().start()
    for k in range(8):
        norm_copy(k, all_norms[k]).start()
    x_local(1).start()
    x_local(2).start()
    def clear(i, carry):
        l = i // (ROWS * CHIPS)
        r = (i // CHIPS) % ROWS
        b = i % CHIPS

        @pl.when((b > chip) | ((l == 0) & (b < chip - 2)))
        def _():
            kvbuf[l, r, pl.ds(pl.multiple_of(b * CTOK, CTOK), CTOK), HKV:] = jnp.zeros((CTOK, HKV), BF16)
        return carry
    lax.fori_loop(0, 2 * ROWS * CHIPS, clear, 0)
    freq_copy().wait()
    pos_local().wait()
    start_kv(wk0, wv0, 0)
    with jax.named_scope("tables"):
        tables(core)
    barrier = pltpu.get_barrier_semaphore()
    for k in range(1, 8):
        pl.semaphore_signal(barrier, inc=1, device_id=at(lax.rem(me + k, 8)), device_id_type=MESH)
    with jax.named_scope("entry"):
        pl.semaphore_wait(barrier, 7)
    x_remote(0).start()
    for k in range(1, 8):
        pos_remote(k).start()
    for r in range(1, ROWS):
        x_remote(r).start()
    for k in range(8):
        norm_copy(k, all_norms[k]).wait()
    for k in range(8):
        norms[k] = nraw[k][...].reshape(1, DIM)

    @pl.when(core == 0)
    def _():
        pos_remote(7).wait_recv()

    @pl.when(core == 1)
    def _():
        pos_remote(1).wait_recv()
    with jax.named_scope("tables"):
        tables(1 - core)
    start_q(wq0, 1)
    start_wo(me >= 0, 2)

    def first_norm(r, carry):
        with jax.named_scope("x_wait"):
            x_local(r).wait()
            x_remote(r).wait()

        def chunk(i, carry):
            for t in range(0, NCHUNK, PIECE):
                rows = pl.ds(pl.multiple_of(i * NCHUNK + t, PIECE), PIECE)
                hpeer[r // 2, rows, pl.ds(pl.multiple_of((r % 2) * DIM, DIM), DIM)] = rms(
                    xbuf[r, rows, :].astype(F32), norms[0])
            return carry
        lax.fori_loop(0, CTOK // NCHUNK, chunk, 0)
        return carry

    start_gu(me >= 0, 0, 3)
    wait_w(0)

    def a0(r):
        return hpeer[r // 2, :, pl.ds(pl.multiple_of((r % 2) * DIM, DIM), DIM)]

    def first_kv(r, carry):
        first_norm(r, 0)
        kv_part(lambda: a0(r), 0, 0, r)
        send_kv0(r)
        return carry
    with jax.named_scope("first_kv"):
        lax.fori_loop(0, ROWS, first_kv, 0)
    start_gu(me >= 0, 1, 0)
    wait_w(1)

    def first_q(r, carry):
        q_part(lambda: a0(r), 1, r)

        @pl.when(r == 1)
        def _():
            forward(0, 0)
        return carry
    with jax.named_scope("first_q"):
        lax.fori_loop(0, ROWS, first_q, 0)
    start_gu(me >= 0, 2, 1)
    for k in range(1, 8):
        pos_remote(k).wait_send()

    @pl.when(core == 0)
    def _():
        for k in range(1, 7):
            pos_remote(k).wait_recv()

    @pl.when(core == 1)
    def _():
        for k in range(2, 8):
            pos_remote(k).wait_recv()
    attention(0 * me)
    forward(1, 0)
    out_proj(2)
    with jax.named_scope("a_wait"):
        a_remote().wait()

    def first_mid(i, carry):
        mid_rows(0 * me, i * NCHUNK)
        return carry
    lax.fori_loop(0, CTOK // NCHUNK, first_mid, 0)

    def step(j, carry):
        first = j < ROWS
        first_next = j + 1 < ROWS
        more = j + 1 < STEPS
        par = j % 2
        has_qkv = (j >= 1) & (j <= ROWS)
        next_qkv = j + 1 <= ROWS
        done = jnp.where(j >= 1, jnp.minimum(j - 1, ROWS), 0)
        extra = jnp.where(has_qkv, 2, 0)
        sb = 3 + 2 * done
        db = sb + extra + GU
        nxt = jnp.minimum(j + 1, STEPS - 1)

        def sl(p):
            return lax.rem(p, DEPTH)

        def gate_up(i, pos, beside):
            slot = sl(pos)
            with jax.named_scope("gu_wait"):
                wait_w(slot)
            base = i * 512
            prev = base - 256 if not isinstance(i, int) or i > 0 else base + 256
            hown[:, pl.ds(pl.multiple_of(prev, 256), 256)] = gated(gs[...], us[...])
            g = dot(mbuf[...], unit(slot, 0))
            u = dot(mbuf[...], unit(slot, 1))
            beside()
            hown[:, pl.ds(pl.multiple_of(base, 256), 256)] = gated(g, u)
            gs[...] = dot(mbuf[...], unit(slot, 2))
            us[...] = dot(mbuf[...], unit(slot, 3))

        @pl.when(has_qkv)
        def _():
            start_q(wq1, sl(sb + 3))

        @pl.when(jnp.logical_not(has_qkv))
        def _():
            start_gu(first, 3, sl(sb + 3))
        with jax.named_scope("gate_up0"):
            gate_up(0, sb, lambda: None)

        @pl.when(has_qkv)
        def _():
            start_gu(first, 2, sl(sb + 4))

        @pl.when(jnp.logical_not(has_qkv))
        def _():
            start_gu(first, 4, sl(sb + 4))

        @pl.when(j >= 1)
        def _():
            with jax.named_scope("d_wait"):
                d_remote(1 - par).wait()
        last = jnp.maximum(j - 1, 0)

        def ending():
            for c in range(2):
                end_rows(last, 1 - par, c * NCHUNK, j >= 1)
        with jax.named_scope("gate_up1"):
            gate_up(1, sb + 1, ending)

        @pl.when(has_qkv)
        def _():
            start_gu(first, 3, sl(sb + 5))
            wait_w(sl(sb + 2))
            with jax.named_scope("kv"):
                kv_part(lambda: dbuf[1 - par], sl(sb + 2), 1, last)
            send_kv(1, last, 3)
            start_gu(first, 4, sl(sb + 6))
            wait_w(sl(sb + 3))
            with jax.named_scope("q"):
                q_part(lambda: dbuf[1 - par], sl(sb + 3), last)

        @pl.when(j > ROWS)
        def _():
            put_out(j - 1).start()

        @pl.when(more)
        def _():
            with jax.named_scope("att_wait"):
                @pl.when(j == 0)
                def _():
                    forward(1, 1)

                @pl.when(j == 1)
                def _():
                    forward(2, 1)
                kv_wait(j + 1)

        def scoring(i, carry):
            pos = sb + extra + i

            @pl.when(i + 3 < GU)
            def _():
                start_gu(first, i + 3, sl(pos + 3))

            @pl.when(i + 3 >= GU)
            def _():
                start_down(first, i + 3 - GU, sl(pos + 3))
            h_remote(par, i - 2).start()
            e = i - 2
            gate_up(i, pos, lambda: score(nxt, e // CHIPS, e % CHIPS))
            return carry
        with jax.named_scope("gate_up"):
            lax.fori_loop(2, GU, scoring, 0)

        hown[:, FFH - 256:FFH] = gated(gs[...], us[...])
        h_remote(par, GU - 2).start()
        h_remote(par, GU - 1).start()

        @pl.when(j == 0)
        def _():
            forward(2, 0)

        def down_col(n):
            return pl.ds(pl.multiple_of(core * DH + n * 256, 256), 256)

        mine = pl.ds(pl.multiple_of(core * FFH, FFH), FFH)
        other = pl.ds(pl.multiple_of((1 - core) * FFH, FFH), FFH)
        with jax.named_scope("down_a"):
            @pl.when(more)
            def _():
                start_wo(first_next, sl(db + 3))

            @pl.when(jnp.logical_not(more))
            def _():
                start_down(first, 3, sl(db + 3))
            wait_w(sl(db))
            wait_w(sl(db + 1))
            gs[...] = dot(hown[...], ring[sl(db), mine, :])
            mix(nxt, 0)
            us[...] = dot(hown[...], ring[sl(db + 1), mine, :])
            mix(nxt, 1)

            @pl.when(more)
            def _():
                o_remote().start()
            with jax.named_scope("h_wait"):
                h_all(par).wait()
            gb[...] = dot(hpeer[par], ring[sl(db), other, :])
            ub[...] = dot(hpeer[par], ring[sl(db + 1), other, :])
            dbuf[par, :, down_col(0)] = (gs[...] + gb[...]).astype(BF16)
            dbuf[par, :, down_col(1)] = (us[...] + ub[...]).astype(BF16)

        @pl.when(more)
        def _():
            start_down(first, 3, sl(db + 4))
            start_down(first, 4, sl(db + 5))

        @pl.when(jnp.logical_not(more))
        def _():
            start_down(first, 4, sl(db + 4))
        with jax.named_scope("down2"):
            wait_w(sl(db + 2))
            gs[...] = dot(hown[...], ring[sl(db + 2), mine, :])
            us[...] = dot(hpeer[par], ring[sl(db + 2), other, :])
            dbuf[par, :, down_col(2)] = (gs[...] + us[...]).astype(BF16)

        @pl.when(more)
        def _():
            start_gu(first_next, 0, sl(db + 6))
            with jax.named_scope("proj"):
                out_proj(sl(db + 3))
            start_gu(first_next, 1, sl(db + 7))
        s3 = sl(db + 3 + jnp.where(more, 1, 0))
        s4 = sl(db + 4 + jnp.where(more, 1, 0))
        with jax.named_scope("down3"):
            wait_w(s3)
            wait_w(s4)
            gs[...] = dot(hown[...], ring[s3, mine, :])
            us[...] = dot(hown[...], ring[s4, mine, :])

        @pl.when(more)
        def _():
            with jax.named_scope("a_wait"):
                a_remote().wait()

        with jax.named_scope("down4"):
            gb[...] = dot(hpeer[par], ring[s3, other, :])
            ub[...] = dot(hpeer[par], ring[s4, other, :])
            for c in range(2):
                mid_rows(nxt, c * NCHUNK, more)
            dbuf[par, :, down_col(3)] = (gs[...] + gb[...]).astype(BF16)
            dbuf[par, :, down_col(4)] = (us[...] + ub[...]).astype(BF16)

        @pl.when(more)
        def _():
            @pl.when(next_qkv)
            def _():
                start_kv(wk1, wv1, sl(db + 8))

            @pl.when(jnp.logical_not(next_qkv))
            def _():
                start_gu(first_next, 2, sl(db + 8))
        d_remote(par).start()
        return carry

    lax.fori_loop(0, STEPS, step, 0)

    d_remote((STEPS - 1) % 2).wait()

    def final(i, carry):
        end_rows(STEPS - 1 + 0 * me, (STEPS - 1) % 2, core * TOK + i * NCHUNK)
        return carry
    lax.fori_loop(0, TOK // NCHUNK, final, 0)
    put_out(STEPS - 1).start()
    for r in range(ROWS):
        put_out(r).wait()
    for r in range(ROWS):
        for d in range(1, CHIPS):
            @pl.when(chip + d < CHIPS)
            def _(r=r, d=d):
                kv_remote(1, r, d).wait_send()

        @pl.when(chip == 0)
        def _(r=r):
            kv_remote(0, r, 2).wait_send()

        @pl.when((chip == 0) | (chip == 2))
        def _(r=r):
            kv_remote(0, r, 1).wait_send()

        @pl.when(chip == 1)
        def _(r=r):
            for h in range(2):
                kv_second(r, h).wait_send()

        @pl.when(chip == 3)
        def _(r=r):
            for h in range(2):
                kv_relay(r, h).wait_send()


def solution(mesh):
    def device_step(hidden, positions, *weights):
        local_w = weights[:11]
        global_w = weights[11:]
        half_dim = HEAD_DIM // 2
        inv_freq = (THETA ** (-(np.arange(half_dim, dtype=np.float64) * 2.0 / HEAD_DIM))).astype(np.float32)
        freq = jnp.asarray(inv_freq.reshape(1, half_dim))
        norms = local_w[7:11] + global_w[7:11]
        hbm = pl.BlockSpec(memory_space=pltpu.HBM)
        dma = pltpu.SemaphoreType.DMA
        flops = 2 * ROWS * TOK * 2 * (DIM * 4096 + 2048 * DIM + 3 * DIM * FF)
        return pl.pallas_call(
            kernel,
            out_shape=jax.ShapeDtypeStruct(hidden.shape, hidden.dtype),
            in_specs=[hbm] * 25,
            out_specs=hbm,
            scratch_shapes=[
                pltpu.VMEM((DEPTH, FF, 256), BF16),
                pltpu.VMEM((2, ROWS, KEYS, 2 * HKV), BF16),
                pltpu.VMEM((ROWS, CTOK, DIM), BF16),
                pltpu.VMEM((CTOK, DIM), BF16),
                pltpu.VMEM((CTOK, FFH), BF16),
                pltpu.VMEM((2, CTOK, FFH), BF16),
                pltpu.VMEM((ROWS, 4, CTOK, HEAD_DIM), BF16),
                pltpu.VMEM((CTOK, 2 * HQ), BF16),
                pltpu.VMEM((CTOK, DIM), BF16),
                pltpu.VMEM((2, CTOK, DIM), BF16),
                pltpu.VMEM((2, ROWS, TOK, 128), F32),
                pltpu.VMEM((2, ROWS, TOK, 128), F32),
                pltpu.VMEM((2, ROWS, TOK, 128), jnp.int32),
                pltpu.VMEM((8, ROWS, 128), jnp.int32),
                pltpu.VMEM((1, 128), F32),
                pltpu.VMEM((8, 1, DIM), F32),
                *[pltpu.VMEM((DIM,), F32)] * 8,
                pltpu.VMEM((4, CTOK, KEYS), F32),
                pltpu.VMEM((4, CTOK, 128), F32),
                *[pltpu.VMEM((CTOK, 256), F32)] * 4,
                dma((9,)), dma((DEPTH,)), dma((ROWS,)), dma((ROWS,)), dma((ROWS,)),
                dma((8,)), dma((8,)),
                dma((2, ROWS, CHIPS)), dma((2, ROWS, CHIPS)), dma((ROWS, 2)), dma((ROWS, 2)),
                dma, dma, dma, dma,
                dma((2,)), dma((2,)), dma((2,)), dma((2,)), dma((ROWS,)),
            ],
            compiler_params=pltpu.CompilerParams(
                collective_id=0, has_side_effects=True, vmem_limit_bytes=67043328),
            cost_estimate=pl.CostEstimate(flops=flops, bytes_accessed=600000000, transcendentals=0),
            name="layers",
        )(hidden, positions, freq, *norms, *local_w[:7], *global_w[:7])

    specs_in = tuple([P("dp", "cp"), P("dp", "cp")] + [P()] * 22)
    return jax.shard_map(device_step, mesh=mesh, in_specs=specs_in, out_specs=P("dp", "cp"), check_vma=False)
```

time: 313 us -> 239 us (0.76)
  Pallas kernels: 300 us -> 236 us
  local copies, waits for them, and re-layouts: 10.1 us -> 2.94 us
    pallas_call x1, Pallas kernels: 300 us -> 236 us  [device_step(): pl.pallas_call(kernel, out_shape=jax.ShapeDtypeStruct(hidden.shape, hidde...]
    another operation x9 -> x0, local copies, waits for them, and re-layouts: 6.46 us -> none  [device_step(): norms = jnp.stack(local_w[7:11] + global_w[7:11])]
where the time goes in v2:
time: 239 us
  Pallas kernels  236 us (99%)
  local copies, waits for them, and re-layouts  2.94 us (1%)
    pallas_call x1, Pallas kernels, device_step(): pl.pallas_call(kernel, out_shape=jax.ShapeDtypeStruct(hidden.shape, hidde...  236 us

profile of v2, /device:TPU:5, one launch (start us, length us, event | category | flops | bytes accessed | tf_op | source)
XLA Modules:
  0.0 238.7 jit_solution(17561002221629854395)
XLA Ops:
  0.0 235.7 %layers.1 = bf16[3,128,2560]{2,1,0:T(8,128)(2,1)} custom-call(bf16[3,128,2560]{2,1,0:T(8,128)(2,1)} %x_hbm.1, s32[3,128]{1,0:T(4,128)} %pos_in.1, f32[1,128]{1,0:T(1,128)} %constant.2.clone.freq_in, f32[2560]{0:T(1024)} %n0.1, f32[2560]{0:T(1024)} %n1.1, f32[2560]{0:T(1024)} %n2.1, f32[2560]{0:T(1024)} %n3.1, f32[2560]{0:T(1024)} %n4.1, f32[2560]{0:T(1024)} %n5.1, ...), custom_call_target="tpu_custom_call" | custom-call | flops 144955146240 | bytes 600000000 | tf_op jit(solution)/shard_map/layers/pallas_call | solution.py:720
  235.7 2.9 %copy.27 = bf16[3,128,2560]{2,1,0:T(8,128)(2,1)} copy(bf16[3,128,2560]{2,1,0:T(8,128)(2,1)} %layers.1) | data formatting | bytes 3932160

commit v3 on v2

--- a/solution.py
+++ b/solution.py
@@ -36,6 +36,8 @@
 SCORES = 8
 NCHUNK = 128
 PIECE = 16
+PIECES = 4
+PTOK = CTOK // PIECES
 KEYS = CHIPS * CTOK
 
 
@@ -58,7 +60,7 @@
            wq0, wk0, wv0, wo0, wg0, wu0, wd0, wq1, wk1, wv1, wo1, wg1, wu1, wd1,
            out_hbm,
            ring, kvbuf, xbuf, mbuf, hown, hpeer, qbuf, obuf, abuf, dbuf, cosb, sinb, tposb, posbuf, freq, norms, r0, r1, r2, r3, r4, r5, r6, r7, ebuf, sbuf, gs, us, gb, ub,
-           n_sem, ring_sem, xl_sem, xs_sem, xr_sem, ps_sem, pr_sem, kvs_sem, kvr_sem, ks_sem, kr_sem,
+           n_sem, ring_sem, half_sem, xl_sem, xs_sem, xr_sem, ps_sem, pr_sem, kvs_sem, kvr_sem, ks_sem, kr_sem,
            os_sem, or_sem, as_sem, ar_sem, hs_sem, hr_sem, dss_sem, dr_sem, out_sem):
     me = lax.axis_index("cp")
     chip = me // 2
@@ -161,7 +163,7 @@
             device_id=at(lax.rem(me + 2 * d, 8)), device_id_type=MESH)
 
     def kv_piece(r, h):
-        return kvbuf.at[0, r, pl.ds(pl.multiple_of(CTOK + h * TOK, TOK), TOK), :]
+        return kvbuf.at[0, r, pl.ds(pl.multiple_of(CTOK + h * PTOK, PTOK), PTOK), :]
 
     def kv_second(r, h):
         return pltpu.make_async_remote_copy(
@@ -187,7 +189,7 @@
 
         @pl.when(chip == 1)
         def _():
-            for h in range(2):
+            for h in range(PIECES):
                 kv_second(r, h).start()
 
         @pl.when(chip == 2)
@@ -197,9 +199,10 @@
     def half(buf, width):
         return buf.at[:, pl.ds(pl.multiple_of(core * width, 256), width)]
 
-    def o_remote():
-        return pltpu.make_async_remote_copy(
-            half(obuf, HQ), half(obuf, HQ), os_sem, or_sem, device_id=at(peer), device_id_type=MESH)
+    def o_remote(kh):
+        cols = obuf.at[:, pl.ds(pl.multiple_of(core * HQ + kh * 512, 512), 512)]
+        return pltpu.make_async_remote_copy(
+            cols, cols, os_sem.at[kh], or_sem.at[kh], device_id=at(peer), device_id_type=MESH)
 
     def a_remote():
         return pltpu.make_async_remote_copy(
@@ -273,10 +276,10 @@
             @pl.when(chip == 2)
             def _():
                 kv_remote(0, r, 2).wait_recv()
-                for h in range(2):
+                for h in range(PIECES):
                     kv_relay(r, h).wait_recv()
 
-    def score(j, kh, t):
+    def score(j, kh, t, fresh):
         l = j // ROWS
         r = j % ROWS
         reach = WINDOW + l * 1000000
@@ -292,7 +295,7 @@
             e = jnp.exp2(EXP2_CAP * jnp.tanh(s * (1.0 / SOFT_CAP)))
             for c in range(2):
                 rows = slice(c * TOK, (c + 1) * TOK)
-                tot = jnp.where(t == 0, 0.0, sbuf[2 * kh + hh, rows, :])
+                tot = jnp.where(fresh, 0.0, sbuf[2 * kh + hh, rows, :])
                 for kc in range(2):
                     piece = jnp.where(masks[c, kc], e[rows, kc * 128:(kc + 1) * 128], 0.0)
                     ebuf[2 * kh + hh, rows, pl.ds(pl.multiple_of(t * CTOK + kc * 128, 128), 128)] = piece
@@ -309,25 +312,47 @@
             col = pl.multiple_of(core * HQ + (2 * kh + hh) * 256, 256)
             obuf[:, pl.ds(col, 256)] = dot(p, v).astype(BF16)
 
-    def attention(j):
+    def attention():
+        zero = 0 * me
+
+        def block(t, fresh):
+            def go(kh, carry):
+                score(zero, kh, t, fresh)
+                return carry
+            with jax.named_scope("att"):
+                lax.fori_loop(0, 2, go, 0)
+
+        def hop(d):
+            return lax.rem(chip + CHIPS - d, CHIPS)
+        block(chip, me >= 0)
+        block(hop(3), me < 0)
         with jax.named_scope("att_wait"):
-            forward(0, 1)
-            kv_wait(j)
+            @pl.when(chip == 2)
+            def _():
+                kv_remote(0, zero, 2).wait_recv()
+            forward(0, 3)
+        block(hop(2), me < 0)
+        with jax.named_scope("att_wait"):
+            @pl.when((chip == 1) | (chip == 3))
+            def _():
+                kv_remote(0, zero, 1).wait_recv()
+
+            @pl.when(chip == 2)
+            def _():
+                for h in range(PIECES):
+                    kv_relay(zero, h).wait_recv()
+        block(hop(1), me < 0)
         with jax.named_scope("att"):
-            def go(i, carry):
-                score(j, i // CHIPS, i % CHIPS)
-                return carry
-            lax.fori_loop(0, SCORES, go, 0)
-
-            def go2(i, carry):
-                mix(j, i)
+            def go2(kh, carry):
+                mix(zero, kh)
+                o_remote(kh).start()
                 return carry
             lax.fori_loop(0, 2, go2, 0)
-        o_remote().start()
 
     def out_proj(slot):
         with jax.named_scope("o_wait"):
-            o_remote().wait()
+            for kh in range(2):
+                o_remote(kh).wait()
         with jax.named_scope("wo_wait"):
             wait_w(slot)
         for t in range(5):
@@ -444,10 +469,11 @@
     def first_q(r, carry):
         q_part(lambda: a0(r), 1, r)
 
-        @pl.when(r == 1)
-        def _():
-            forward(0, 0)
+        @pl.when(r >= 1)
+        def _():
+            forward(0, r)
         return carry
+    forward(0, 0)
     with jax.named_scope("first_q"):
         lax.fori_loop(0, ROWS, first_q, 0)
     start_gu(me >= 0, 2, 1)
@@ -463,9 +489,11 @@
     def _():
         for k in range(2, 8):
             pos_remote(k).wait_recv()
-    attention(0 * me)
+    attention()
     forward(1, 0)
+    forward(1, 1)
     out_proj(2)
+    forward(1, 2)
     with jax.named_scope("a_wait"):
         a_remote().wait()
 
@@ -473,6 +501,7 @@
         mid_rows(0 * me, i * NCHUNK)
         return carry
     lax.fori_loop(0, CTOK // NCHUNK, first_mid, 0)
+    forward(1, 3)
 
     def step(j, carry):
         first = j < ROWS
@@ -480,7 +509,6 @@
         more = j + 1 < STEPS
         par = j % 2
         has_qkv = (j >= 1) & (j <= ROWS)
-        next_qkv = j + 1 <= ROWS
         done = jnp.where(j >= 1, jnp.minimum(j - 1, ROWS), 0)
         extra = jnp.where(has_qkv, 2, 0)
         sb = 3 + 2 * done
@@ -553,13 +581,6 @@
         @pl.when(more)
         def _():
             with jax.named_scope("att_wait"):
-                @pl.when(j == 0)
-                def _():
-                    forward(1, 1)
-
-                @pl.when(j == 1)
-                def _():
-                    forward(2, 1)
                 kv_wait(j + 1)
 
         def scoring(i, carry):
@@ -574,7 +595,7 @@
                 start_down(first, i + 3 - GU, sl(pos + 3))
             h_remote(par, i - 2).start()
             e = i - 2
-            gate_up(i, pos, lambda: score(nxt, e // CHIPS, e % CHIPS))
+            gate_up(i, pos, lambda: score(nxt, e // CHIPS, e % CHIPS, e % CHIPS == 0))
             return carry
         with jax.named_scope("gate_up"):
             lax.fori_loop(2, GU, scoring, 0)
@@ -585,13 +606,36 @@
 
         @pl.when(j == 0)
         def _():
-            forward(2, 0)
+            for h in range(PIECES):
+                forward(2, h)
 
         def down_col(n):
             return pl.ds(pl.multiple_of(core * DH + n * 256, 256), 256)
 
         mine = pl.ds(pl.multiple_of(core * FFH, FFH), FFH)
         other = pl.ds(pl.multiple_of((1 - core) * FFH, FFH), FFH)
+        def pair(lhs, sa, sb_, rows, out_a, out_b):
+            y = dot(lhs, jnp.concatenate([ring[sa, rows, :], ring[sb_, rows, :]], axis=1))
+            out_a[...] = y[:, :256]
+            out_b[...] = y[:, 256:]
+
+        def half_down(n, pos, k):
+            row = pl.multiple_of((core + k - 2 * core * k) * FFH, FFH)
+
+            def go(wd):
+                pltpu.make_async_copy(
+                    wd.at[pl.ds(row, FFH), pl.ds(pl.multiple_of(core * DH + n * 256, 256), 256)],
+                    ring.at[sl(pos), pl.ds(row, FFH), :], half_sem.at[k, n - 3]).start()
+            by_layer(first, lambda: go(wd0), lambda: go(wd1))
+
+        def half_wait(n, pos, k):
+            row = pl.multiple_of((core + k - 2 * core * k) * FFH, FFH)
+            pltpu.make_async_copy(
+                wd0.at[pl.ds(row, FFH), pl.ds(0, 256)], ring.at[sl(pos), pl.ds(row, FFH), :],
+                half_sem.at[k, n - 3]).wait()
+
+        p3 = db + 3 + jnp.where(more, 1, 0)
+        p4 = p3 + 1
         with jax.named_scope("down_a"):
             @pl.when(more)
             def _():
@@ -599,32 +643,31 @@
 
             @pl.when(jnp.logical_not(more))
             def _():
-                start_down(first, 3, sl(db + 3))
+                half_down(3, p3, 0)
+                half_down(3, p3, 1)
             wait_w(sl(db))
             wait_w(sl(db + 1))
-            gs[...] = dot(hown[...], ring[sl(db), mine, :])
+            pair(hown[...], sl(db), sl(db + 1), mine, gs, us)
             mix(nxt, 0)
-            us[...] = dot(hown[...], ring[sl(db + 1), mine, :])
-            mix(nxt, 1)
 
             @pl.when(more)
             def _():
-                o_remote().start()
+                o_remote(0).start()
+                half_down(3, p3, 0)
+            half_down(4, p4, 0)
             with jax.named_scope("h_wait"):
                 h_all(par).wait()
-            gb[...] = dot(hpeer[par], ring[sl(db), other, :])
-            ub[...] = dot(hpeer[par], ring[sl(db + 1), other, :])
+            pair(hpeer[par], sl(db), sl(db + 1), other, gb, ub)
+            mix(nxt, 1)
             dbuf[par, :, down_col(0)] = (gs[...] + gb[...]).astype(BF16)
             dbuf[par, :, down_col(1)] = (us[...] + ub[...]).astype(BF16)
 
-        @pl.when(more)
-        def _():
-            start_down(first, 3, sl(db + 4))
-            start_down(first, 4, sl(db + 5))
-
-        @pl.when(jnp.logical_not(more))
-        def _():
-            start_down(first, 4, sl(db + 4))
+            @pl.when(more)
+            def _():
+                o_remote(1).start()
+                half_down(3, p3, 1)
+            half_down(4, p4, 1)
+
         with jax.named_scope("down2"):
             wait_w(sl(db + 2))
             gs[...] = dot(hown[...], ring[sl(db + 2), mine, :])
@@ -637,13 +680,13 @@
             with jax.named_scope("proj"):
                 out_proj(sl(db + 3))
             start_gu(first_next, 1, sl(db + 7))
-        s3 = sl(db + 3 + jnp.where(more, 1, 0))
-        s4 = sl(db + 4 + jnp.where(more, 1, 0))
+        s3 = sl(p3)
+        s4 = sl(p4)
         with jax.named_scope("down3"):
-            wait_w(s3)
-            wait_w(s4)
-            gs[...] = dot(hown[...], ring[s3, mine, :])
-            us[...] = dot(hown[...], ring[s4, mine, :])
+            with jax.named_scope("dn_wait"):
+                half_wait(3, p3, 0)
+                half_wait(4, p4, 0)
+            pair(hown[...], s3, s4, mine, gs, us)
 
         @pl.when(more)
         def _():
@@ -651,8 +694,10 @@
                 a_remote().wait()
 
         with jax.named_scope("down4"):
-            gb[...] = dot(hpeer[par], ring[s3, other, :])
-            ub[...] = dot(hpeer[par], ring[s4, other, :])
+            with jax.named_scope("dn_wait"):
+                half_wait(3, p3, 1)
+                half_wait(4, p4, 1)
+            pair(hpeer[par], s3, s4, other, gb, ub)
             for c in range(2):
                 mid_rows(nxt, c * NCHUNK, more)
             dbuf[par, :, down_col(3)] = (gs[...] + gb[...]).astype(BF16)
@@ -660,11 +705,11 @@
 
         @pl.when(more)
         def _():
-            @pl.when(next_qkv)
+            @pl.when(j + 1 <= ROWS)
             def _():
                 start_kv(wk1, wv1, sl(db + 8))
 
-            @pl.when(jnp.logical_not(next_qkv))
+            @pl.when(j + 1 > ROWS)
             def _():
                 start_gu(first_next, 2, sl(db + 8))
         d_remote(par).start()
@@ -697,12 +742,12 @@
 
         @pl.when(chip == 1)
         def _(r=r):
-            for h in range(2):
+            for h in range(PIECES):
                 kv_second(r, h).wait_send()
 
         @pl.when(chip == 3)
         def _(r=r):
-            for h in range(2):
+            for h in range(PIECES):
                 kv_relay(r, h).wait_send()
 
 
@@ -743,10 +788,10 @@
                 pltpu.VMEM((4, CTOK, KEYS), F32),
                 pltpu.VMEM((4, CTOK, 128), F32),
                 *[pltpu.VMEM((CTOK, 256), F32)] * 4,
-                dma((9,)), dma((DEPTH,)), dma((ROWS,)), dma((ROWS,)), dma((ROWS,)),
+                dma((9,)), dma((DEPTH,)), dma((2, 2)), dma((ROWS,)), dma((ROWS,)), dma((ROWS,)),
                 dma((8,)), dma((8,)),
-                dma((2, ROWS, CHIPS)), dma((2, ROWS, CHIPS)), dma((ROWS, 2)), dma((ROWS, 2)),
-                dma, dma, dma, dma,
+                dma((2, ROWS, CHIPS)), dma((2, ROWS, CHIPS)), dma((ROWS, PIECES)), dma((ROWS, PIECES)),
+                dma((2,)), dma((2,)), dma, dma,
                 dma((2,)), dma((2,)), dma((2,)), dma((2,)), dma((ROWS,)),
             ],
             compiler_params=pltpu.CompilerParams(

time: 239 us -> 230 us (0.962)
  Pallas kernels: 236 us -> 227 us
    pallas_call x1, Pallas kernels: 236 us -> 227 us  [device_step(): pl.pallas_call(kernel, out_shape=jax.ShapeDtypeStruct(hidden.shape, hidde...]
where the time goes in v3:
time: 230 us
  Pallas kernels  227 us (99%)
  local copies, waits for them, and re-layouts  2.94 us (1%)
    pallas_call x1, Pallas kernels, device_step(): pl.pallas_call(kernel, out_shape=jax.ShapeDtypeStruct(hidden.shape, hidde...  227 us

profile of v3, /device:TPU:5, one launch (start us, length us, event | category | flops | bytes accessed | tf_op | source)
XLA Modules:
  0.0 230.0 jit_solution(14687910224994512845)
XLA Ops:
  0.0 227.1 %layers.1 = bf16[3,128,2560]{2,1,0:T(8,128)(2,1)} custom-call(bf16[3,128,2560]{2,1,0:T(8,128)(2,1)} %x_hbm.1, s32[3,128]{1,0:T(4,128)} %pos_in.1, f32[1,128]{1,0:T(1,128)} %constant.2.clone.freq_in, f32[2560]{0:T(1024)} %n0.1, f32[2560]{0:T(1024)} %n1.1, f32[2560]{0:T(1024)} %n2.1, f32[2560]{0:T(1024)} %n3.1, f32[2560]{0:T(1024)} %n4.1, f32[2560]{0:T(1024)} %n5.1, ...), custom_call_target="tpu_custom_call" | custom-call | flops 144955146240 | bytes 600000000 | tf_op jit(solution)/shard_map/layers/pallas_call | solution.py:765
  227.1 2.9 %copy.27 = bf16[3,128,2560]{2,1,0:T(8,128)(2,1)} copy(bf16[3,128,2560]{2,1,0:T(8,128)(2,1)} %layers.1) | data formatting | bytes 3932160
